TPU v7x, 32 devices: a whole 2x2x4 slice. The times are simulated.
32 devices in a mesh: rep: 4 (over y, x), fsdp: 4 (over z), seq: 2 (over core).
Axes of the slice: x: 2, y: 2, z: 4, core: 2. Of those that a mesh axis runs over, the one named last changes fastest.
Arguments:
- layer_input: bfloat16 [2, 16, 1024, 768], P(None, ('rep', 'fsdp'), 'seq'), may hold values from -6 to 6
- segment: int32 [2, 16, 1024], P(None, ('rep', 'fsdp')), may hold values from 0 to 3, never falling along the last dimension, each value on 1 to 512 neighbouring positions
- rand_blocks: int32 [2, 16, 12, 16, 3], P(None, ('rep', 'fsdp')), may hold values from 0 to 15
- first_gain: bfloat16 [768], P('fsdp'), may hold values from 0.099609375 to 1.8984375
- first_bias: bfloat16 [768], P('fsdp'), may hold values from -1.75 to 1.75
- query_weight: bfloat16 [768, 768], P('fsdp'), may hold values from -0.21875 to 0.21875
- query_bias: bfloat16 [768], P('fsdp'), may hold values from -1.75 to 1.75
- key_weight: bfloat16 [768, 768], P('fsdp'), may hold values from -0.21875 to 0.21875
- value_weight: bfloat16 [768, 768], P('fsdp'), may hold values from -0.21875 to 0.21875
- value_bias: bfloat16 [768], P('fsdp'), may hold values from -1.75 to 1.75
- out_weight: bfloat16 [768, 768], P('fsdp'), may hold values from -1.75 to 1.75
- out_bias: bfloat16 [768], P('fsdp'), may hold values from -1.75 to 1.75
- second_gain: bfloat16 [768], P('fsdp'), may hold values from 0.099609375 to 1.8984375
- second_bias: bfloat16 [768], P('fsdp'), may hold values from -1.75 to 1.75
- up_weight: bfloat16 [768, 3072], P('fsdp'), may hold values from -0.21875 to 0.21875
- up_bias: bfloat16 [3072], P('fsdp'), may hold values from -1.75 to 1.75
- down_weight: bfloat16 [3072, 768], P('fsdp'), may hold values from -0.21875 to 0.21875
- down_bias: bfloat16 [768], P('fsdp'), may hold values from -1.75 to 1.75
- cotangent: bfloat16 [2, 16, 1024, 768], P(None, ('rep', 'fsdp'), 'seq'), may hold values from -6 to 6
Outputs:
- layer_output: bfloat16 [2, 16, 1024, 768], P(None, ('rep', 'fsdp'), 'seq')
- input_grad: bfloat16 [2, 16, 1024, 768], P(None, ('rep', 'fsdp'), 'seq')
- first_gain_grad: float32 [768], P('fsdp')
- first_bias_grad: float32 [768], P('fsdp')
- query_weight_grad: float32 [768, 768], P('fsdp')
- query_bias_grad: float32 [768], P('fsdp')
- key_weight_grad: float32 [768, 768], P('fsdp')
- value_weight_grad: float32 [768, 768], P('fsdp')
- value_bias_grad: float32 [768], P('fsdp')
- out_weight_grad: float32 [768, 768], P('fsdp')
- out_bias_grad: float32 [768], P('fsdp')
- second_gain_grad: float32 [768], P('fsdp')
- second_bias_grad: float32 [768], P('fsdp')
- up_weight_grad: float32 [768, 3072], P('fsdp')
- up_bias_grad: float32 [3072], P('fsdp')
- down_weight_grad: float32 [3072, 768], P('fsdp')
- down_bias_grad: float32 [768], P('fsdp')
Inputs may be any that keep to these rules, and one draw needn't show every extreme that they name: segment numbers of a sequence never fall; each document is one run of tokens.
All inputs are finite; a program needn't handle non-finite values.
Results may differ from a plain program's by a relative error of at most 0.02.
Values may be sent and summed in bfloat16 or wider, within the bound.
A program may use at most 192 MiB of HBM per device.

v0:
```python
import jax
import jax.numpy as jnp
from jax import lax
from jax.sharding import PartitionSpec as P

HEADS = 12
HDIM = 64
BLOCK = 64


norm_eps = 1e-05


def as_sent(x):

    def short(part):
        return part.astype(jnp.bfloat16) if part.dtype == jnp.float32 else part

    return jax.tree.map(short, x)


def layer_norm(values, gain_vec, offset):
    centre = values - jnp.mean(values, axis=-1, keepdims=True)
    spread = jnp.mean(centre * centre, axis=-1, keepdims=True)
    return centre * lax.rsqrt(spread + norm_eps) * gain_vec + offset


def gelu_exact(values):
    return jax.nn.gelu(values, approximate=False)


def block_allowed(rand_rows, first_block, count_blocks, block_total):
    blocks = jnp.arange(block_total, dtype=jnp.int32)
    query_blocks = first_block + jnp.arange(count_blocks, dtype=jnp.int32)
    chosen = lax.dynamic_slice_in_dim(rand_rows, first_block, count_blocks, axis=1)
    random_hit = jnp.any(chosen[:, :, :, None] == blocks[None, None, None, :], axis=2)
    near_hit = jnp.abs(query_blocks[:, None] - blocks[None, :]) <= 1
    global_hit = (
        (blocks[None, :] == 0)
        | (blocks[None, :] == block_total - 1)
        | (query_blocks[:, None] == 0)
        | (query_blocks[:, None] == block_total - 1)
    )
    return random_hit | (near_hit | global_hit)[None]


def token_allowed(rand_rows, segments, first_row, count_rows, block_size):
    block_total = segments.shape[0] // block_size
    allowed = block_allowed(
        rand_rows, first_row // block_size, count_rows // block_size, block_total
    )
    head_count = allowed.shape[0]
    expanded = jnp.broadcast_to(
        allowed[:, :, None, :, None],
        (head_count, count_rows // block_size, block_size, block_total, block_size),
    )
    expanded = expanded.reshape(head_count, count_rows, block_total * block_size)
    query_seg = lax.dynamic_slice_in_dim(segments, first_row, count_rows)
    same_doc = query_seg[:, None] == segments[None, :]
    return expanded & same_doc[None]


def by_pairs(values):
    row_count = values.shape[0]
    return jnp.moveaxis(values.reshape(row_count, HEADS // 2, 2, HDIM), 1, 0)


def from_pairs(values):
    return jnp.moveaxis(values, 0, 1).reshape(values.shape[1], HEADS * HDIM)


def on_device(
    layer_input,
    segment,
    rand_blocks,
    first_gain,
    first_bias,
    query_weight,
    query_bias,
    key_weight,
    value_weight,
    value_bias,
    out_weight,
    out_bias,
    second_gain,
    second_bias,
    up_weight,
    up_bias,
    down_weight,
    down_bias,
    cotangent,
):
    micro_count, seq_count, half_len, model_width = layer_input.shape
    rows_all = seq_count * half_len
    row_start = lax.axis_index("seq") * half_len
    shards = (
        first_gain,
        first_bias,
        query_weight,
        query_bias,
        key_weight,
        value_weight,
        value_bias,
        out_weight,
        out_bias,
        second_gain,
        second_bias,
        up_weight,
        up_bias,
        down_weight,
        down_bias,
    )
    collected = tuple((jnp.zeros(element.shape, jnp.float32) for element in shards))
    outputs = []
    input_grads = []
    for micro_step in range(micro_count):
        gathered = (
            lax.all_gather(shards[0], "fsdp", axis=0, tiled=True),
            lax.all_gather(shards[1], "fsdp", axis=0, tiled=True),
            lax.all_gather(shards[2], "fsdp", axis=0, tiled=True),
            lax.all_gather(shards[3], "fsdp", axis=0, tiled=True),
            lax.all_gather(shards[4], "fsdp", axis=0, tiled=True),
            lax.all_gather(shards[5], "fsdp", axis=0, tiled=True),
            lax.all_gather(shards[6], "fsdp", axis=0, tiled=True),
            lax.all_gather(shards[7], "fsdp", axis=0, tiled=True),
            lax.all_gather(shards[8], "fsdp", axis=0, tiled=True),
            lax.all_gather(shards[9], "fsdp", axis=0, tiled=True),
            lax.all_gather(shards[10], "fsdp", axis=0, tiled=True),
            lax.all_gather(shards[11], "fsdp", axis=0, tiled=True),
            lax.all_gather(shards[12], "fsdp", axis=0, tiled=True),
            lax.all_gather(shards[13], "fsdp", axis=0, tiled=True),
            lax.all_gather(shards[14], "fsdp", axis=0, tiled=True),
        )
        (
            gain_one,
            bias_one,
            w_query,
            b_query,
            w_key,
            w_value,
            b_value,
            w_out,
            b_out,
            gain_two,
            bias_two,
            w_up,
            b_up,
            w_down,
            b_down,
        ) = gathered
        tokens = layer_input[micro_step].reshape(rows_all, model_width).astype(jnp.float32)
        normed, norm_one_back = jax.vjp(
            layer_norm, tokens, gain_one.astype(jnp.float32), bias_one.astype(jnp.float32)
        )
        normed = normed.astype(jnp.bfloat16)
        queries = (
            jnp.dot(normed, w_query, preferred_element_type=jnp.float32)
            + b_query.astype(jnp.float32)
        ).astype(jnp.bfloat16)
        keys_own = jnp.dot(normed, w_key, preferred_element_type=jnp.float32).astype(jnp.bfloat16)
        values_own = (
            jnp.dot(normed, w_value, preferred_element_type=jnp.float32)
            + b_value.astype(jnp.float32)
        ).astype(jnp.bfloat16)
        keys_all, values_all = (
            lax.all_gather(
                keys_own.reshape(seq_count, half_len, model_width), "seq", axis=1, tiled=True
            ),
            lax.all_gather(
                values_own.reshape(seq_count, half_len, model_width), "seq", axis=1, tiled=True
            ),
        )
        member = 0
        seg_row = segment[micro_step, member]
        rand_pairs = rand_blocks[micro_step, member].reshape(
            HEADS // 2, 2, rand_blocks.shape[3], rand_blocks.shape[4]
        )
        query_pairs = by_pairs(queries)
        key_pairs = by_pairs(keys_all[member])
        value_pairs = by_pairs(values_all[member])

        def forward_pair(pair_item, seg_row=seg_row):
            query_part, key_part, value_part, rand_part = pair_item
            allowed = token_allowed(rand_part, seg_row, row_start, half_len, BLOCK)
            raw_scores = (
                jnp.einsum("qhd,khd->hqk", query_part, key_part, preferred_element_type=jnp.float32)
                * 0.125
            )
            scores = jnp.where(allowed, raw_scores, -1e30)
            row_peak = jnp.max(scores, axis=-1, keepdims=True)
            shifted = jnp.exp(scores - row_peak)
            row_mass = jnp.sum(shifted, axis=-1, keepdims=True)
            attn_probs = (shifted / row_mass).astype(jnp.bfloat16)
            mixed_part = jnp.einsum(
                "hqk,khd->qhd", attn_probs, value_part, preferred_element_type=jnp.float32
            )
            return (mixed_part, row_peak + jnp.log(row_mass))

        mixed_pair, lse_pair = lax.map(
            forward_pair, (query_pairs, key_pairs, value_pairs, rand_pairs)
        )
        mixed_parts = from_pairs(mixed_pair)
        kept_lse = [lse_pair]
        mixed = mixed_parts.astype(jnp.bfloat16)
        middle = (
            tokens
            + jnp.dot(mixed, w_out, preferred_element_type=jnp.float32)
            + b_out.astype(jnp.float32)
        )
        normed_two, norm_two_back = jax.vjp(
            layer_norm, middle, gain_two.astype(jnp.float32), bias_two.astype(jnp.float32)
        )
        normed_two = normed_two.astype(jnp.bfloat16)
        inner_act = jnp.dot(normed_two, w_up, preferred_element_type=jnp.float32) + b_up.astype(
            jnp.float32
        )
        hidden, gelu_back = jax.vjp(gelu_exact, inner_act)
        hidden = hidden.astype(jnp.bfloat16)
        result = (
            middle
            + jnp.dot(hidden, w_down, preferred_element_type=jnp.float32)
            + b_down.astype(jnp.float32)
        )
        outputs.append(result.astype(jnp.bfloat16).reshape(seq_count, half_len, model_width))
        w_query, w_key, w_value, w_out, w_up, w_down = (
            lax.all_gather(query_weight, "fsdp", axis=0, tiled=True),
            lax.all_gather(key_weight, "fsdp", axis=0, tiled=True),
            lax.all_gather(value_weight, "fsdp", axis=0, tiled=True),
            lax.all_gather(out_weight, "fsdp", axis=0, tiled=True),
            lax.all_gather(up_weight, "fsdp", axis=0, tiled=True),
            lax.all_gather(down_weight, "fsdp", axis=0, tiled=True),
        )
        upstream = cotangent[micro_step].reshape(rows_all, model_width).astype(jnp.float32)
        grad_branch = upstream.astype(jnp.bfloat16)
        grad_w_down = jnp.einsum(
            "rf,rd->fd", hidden, grad_branch, preferred_element_type=jnp.float32
        )
        grad_b_down = jnp.sum(grad_branch, axis=0, dtype=jnp.float32)
        grad_hidden = jnp.einsum(
            "rd,fd->rf", grad_branch, w_down, preferred_element_type=jnp.float32
        )
        grad_inner = gelu_back(grad_hidden)[0].astype(jnp.bfloat16)
        grad_w_up = jnp.einsum(
            "rd,rf->df", normed_two, grad_inner, preferred_element_type=jnp.float32
        )
        grad_b_up = jnp.sum(grad_inner, axis=0, dtype=jnp.float32)
        grad_normed_two = jnp.einsum(
            "rf,df->rd", grad_inner, w_up, preferred_element_type=jnp.float32
        )
        grad_mid_norm, grad_gain_two, grad_bias_two = norm_two_back(grad_normed_two)
        grad_middle = upstream + grad_mid_norm
        grad_attn = grad_middle.astype(jnp.bfloat16)
        grad_w_out = jnp.einsum("rd,re->de", mixed, grad_attn, preferred_element_type=jnp.float32)
        grad_b_out = jnp.sum(grad_attn, axis=0, dtype=jnp.float32)
        grad_mixed = jnp.einsum(
            "re,de->rd", grad_attn, w_out, preferred_element_type=jnp.float32
        ).astype(jnp.bfloat16)
        member = 0
        seg_row = segment[micro_step, member]
        rand_pairs = rand_blocks[micro_step, member].reshape(
            HEADS // 2, 2, rand_blocks.shape[3], rand_blocks.shape[4]
        )
        query_pairs = by_pairs(queries)
        key_pairs = by_pairs(keys_all[member])
        value_pairs = by_pairs(values_all[member])
        grad_pairs = by_pairs(grad_mixed)

        def backward_pair(pair_item, seg_row=seg_row):
            query_part, key_part, value_part, rand_part, grad_part, lse_part = pair_item
            allowed = token_allowed(rand_part, seg_row, row_start, half_len, BLOCK)
            raw_scores = (
                jnp.einsum("qhd,khd->hqk", query_part, key_part, preferred_element_type=jnp.float32)
                * 0.125
            )
            scores = jnp.where(allowed, raw_scores, -1e30)
            attn_probs = jnp.exp(scores - lse_part)
            grad_value_part = jnp.einsum(
                "hqk,qhd->khd",
                attn_probs.astype(jnp.bfloat16),
                grad_part,
                preferred_element_type=jnp.float32,
            )
            grad_probs = jnp.einsum(
                "qhd,khd->hqk", grad_part, value_part, preferred_element_type=jnp.float32
            )
            inner_sum = jnp.sum(attn_probs * grad_probs, axis=-1, keepdims=True)
            grad_scores = (attn_probs * (grad_probs - inner_sum)).astype(jnp.bfloat16)
            grad_query_part = (
                jnp.einsum(
                    "hqk,khd->qhd", grad_scores, key_part, preferred_element_type=jnp.float32
                )
                * 0.125
            )
            grad_key_part = (
                jnp.einsum(
                    "hqk,qhd->khd", grad_scores, query_part, preferred_element_type=jnp.float32
                )
                * 0.125
            )
            return (grad_query_part, grad_key_part, grad_value_part)

        grad_query_pair, grad_key_pair, grad_value_pair = lax.map(
            backward_pair,
            (query_pairs, key_pairs, value_pairs, rand_pairs, grad_pairs, kept_lse[member]),
        )
        query_grads = from_pairs(grad_query_pair)
        key_grads = [from_pairs(grad_key_pair)]
        value_grads = [from_pairs(grad_value_pair)]
        grad_keys_own, grad_values_own = (
            lax.psum_scatter(
                jnp.stack(key_grads).astype(jnp.bfloat16), "seq", scatter_dimension=1, tiled=True
            ).astype(jnp.float32),
            lax.psum_scatter(
                jnp.stack(value_grads).astype(jnp.bfloat16), "seq", scatter_dimension=1, tiled=True
            ).astype(jnp.float32),
        )
        grad_queries = query_grads.astype(jnp.bfloat16)
        grad_keys = grad_keys_own.reshape(rows_all, model_width).astype(jnp.bfloat16)
        grad_values = grad_values_own.reshape(rows_all, model_width).astype(jnp.bfloat16)
        grad_w_query = jnp.einsum(
            "rd,re->de", normed, grad_queries, preferred_element_type=jnp.float32
        )
        grad_b_query = jnp.sum(grad_queries, axis=0, dtype=jnp.float32)
        grad_w_key = jnp.einsum("rd,re->de", normed, grad_keys, preferred_element_type=jnp.float32)
        grad_w_value = jnp.einsum(
            "rd,re->de", normed, grad_values, preferred_element_type=jnp.float32
        )
        grad_b_value = jnp.sum(grad_values, axis=0, dtype=jnp.float32)
        grad_normed = jnp.einsum(
            "re,de->rd", grad_queries, w_query, preferred_element_type=jnp.float32
        )
        grad_normed = grad_normed + jnp.einsum(
            "re,de->rd", grad_keys, w_key, preferred_element_type=jnp.float32
        )
        grad_normed = grad_normed + jnp.einsum(
            "re,de->rd", grad_values, w_value, preferred_element_type=jnp.float32
        )
        grad_tok_norm, grad_gain_one, grad_bias_one = norm_one_back(grad_normed)
        input_grads.append(
            (grad_middle + grad_tok_norm)
            .astype(jnp.bfloat16)
            .reshape(seq_count, half_len, model_width)
        )
        grad_list = (
            grad_gain_one,
            grad_bias_one,
            grad_w_query,
            grad_b_query,
            grad_w_key,
            grad_w_value,
            grad_b_value,
            grad_w_out,
            grad_b_out,
            grad_gain_two,
            grad_bias_two,
            grad_w_up,
            grad_b_up,
            grad_w_down,
            grad_b_down,
        )
        owned_part = (
            lax.psum_scatter(
                grad_list[0].astype(jnp.bfloat16), "fsdp", scatter_dimension=0, tiled=True
            ).astype(jnp.float32),
            lax.psum_scatter(
                grad_list[1].astype(jnp.bfloat16), "fsdp", scatter_dimension=0, tiled=True
            ).astype(jnp.float32),
            lax.psum_scatter(
                grad_list[2].astype(jnp.bfloat16), "fsdp", scatter_dimension=0, tiled=True
            ).astype(jnp.float32),
            lax.psum_scatter(
                grad_list[3].astype(jnp.bfloat16), "fsdp", scatter_dimension=0, tiled=True
            ).astype(jnp.float32),
            lax.psum_scatter(
                grad_list[4].astype(jnp.bfloat16), "fsdp", scatter_dimension=0, tiled=True
            ).astype(jnp.float32),
            lax.psum_scatter(
                grad_list[5].astype(jnp.bfloat16), "fsdp", scatter_dimension=0, tiled=True
            ).astype(jnp.float32),
            lax.psum_scatter(
                grad_list[6].astype(jnp.bfloat16), "fsdp", scatter_dimension=0, tiled=True
            ).astype(jnp.float32),
            lax.psum_scatter(
                grad_list[7].astype(jnp.bfloat16), "fsdp", scatter_dimension=0, tiled=True
            ).astype(jnp.float32),
            lax.psum_scatter(
                grad_list[8].astype(jnp.bfloat16), "fsdp", scatter_dimension=0, tiled=True
            ).astype(jnp.float32),
            lax.psum_scatter(
                grad_list[9].astype(jnp.bfloat16), "fsdp", scatter_dimension=0, tiled=True
            ).astype(jnp.float32),
            lax.psum_scatter(
                grad_list[10].astype(jnp.bfloat16), "fsdp", scatter_dimension=0, tiled=True
            ).astype(jnp.float32),
            lax.psum_scatter(
                grad_list[11].astype(jnp.bfloat16), "fsdp", scatter_dimension=0, tiled=True
            ).astype(jnp.float32),
            lax.psum_scatter(
                grad_list[12].astype(jnp.bfloat16), "fsdp", scatter_dimension=0, tiled=True
            ).astype(jnp.float32),
            lax.psum_scatter(
                grad_list[13].astype(jnp.bfloat16), "fsdp", scatter_dimension=0, tiled=True
            ).astype(jnp.float32),
            lax.psum_scatter(
                grad_list[14].astype(jnp.bfloat16), "fsdp", scatter_dimension=0, tiled=True
            ).astype(jnp.float32),
        )
        collected = tuple((first + second for first, second in zip(collected, owned_part)))
    summed = jax.tree.map(
        lambda part: part.astype(jnp.float32), lax.psum(as_sent(collected), ("rep", "seq"))
    )
    return (jnp.stack(outputs), jnp.stack(input_grads)) + tuple(summed)


def solution(mesh):
    return jax.shard_map(
        on_device,
        mesh=mesh,
        in_specs=(
            P(None, ("rep", "fsdp"), "seq", None),
            P(None, ("rep", "fsdp"), None),
            P(None, ("rep", "fsdp"), None, None, None),
            P("fsdp"),
            P("fsdp"),
            P("fsdp", None),
            P("fsdp"),
            P("fsdp", None),
            P("fsdp", None),
            P("fsdp"),
            P("fsdp", None),
            P("fsdp"),
            P("fsdp"),
            P("fsdp"),
            P("fsdp", None),
            P("fsdp"),
            P("fsdp", None),
            P("fsdp"),
            P(None, ("rep", "fsdp"), "seq", None),
        ),
        out_specs=(
            P(None, ("rep", "fsdp"), "seq", None),
            P(None, ("rep", "fsdp"), "seq", None),
            P("fsdp"),
            P("fsdp"),
            P("fsdp", None),
            P("fsdp"),
            P("fsdp", None),
            P("fsdp", None),
            P("fsdp"),
            P("fsdp", None),
            P("fsdp"),
            P("fsdp"),
            P("fsdp"),
            P("fsdp", None),
            P("fsdp"),
            P("fsdp", None),
            P("fsdp"),
        ),
        check_vma=False,
    )
```

profile of v0, /device:TPU:25, one launch (start us, length us, event | category | flops | bytes accessed | tf_op | source)
XLA Modules:
  0.0 1362.2 jit_solution(6281866680686379533)
XLA Ops:
  17.3 12.8 all-reduce.29
  42.7 27.9 %all-gather.20.cloned.1.call-done = bf16[768,768]{1,0:T(8,128)(2,1)} async-done(((bf16[192,768]{1,0:T(8,128)(2,1)}), bf16[768,768]{1,0:T(8,128)(2,1)}) %all-gather.20.cloned.1.call-update) | async-done | bytes 1179664 | tf_op jit(solution)/shard_map/all_gather | solution.py:122
  81.1 11.4 all-gather.4
  92.4 9.5 all-gather.18.cloned.1.call-done
  118.1 9.8 all-gather.30.cloned.1.call-done
  131.5 72.4 %while.64 = (s32[]{:T(128)}, bf16[6,512,2,64]{1,3,2,0:T(8,128)(2,1)}, f32[6,2,512,1]{2,1,3,0:T(2,128)S(1)}, bf16[6,1024,2,64]{1,3,2,0:T(8,128)(2,1)}, s32[6,2,16...) while((s32[]{:T(128)}, ...), condition=%wide.region_6.7_spmd, body=%wide.region_2.6_spmd.sunk | while | flops 278398272 | bytes 18786792 | solution.py:199
  214.4 72.5 %while.65 = (s32[]{:T(128)}, bf16[6,512,2,64]{1,3,2,0:T(8,128)(2,1)}, f32[6,2,512,1]{2,1,3,0:T(2,128)S(1)}, bf16[6,1024,2,64]{1,3,2,0:T(8,128)(2,1)}, s32[6,2,16...) while((s32[]{:T(128)}, ...), condition=%wide.region_15.16_spmd, body=%wide.region_11.15_spmd.sunk | while | flops 278398272 | bytes 18786792 | solution.py:199
  297.8 34.8 %multiply_convert_fusion.3 = (bf16[512,3072]{1,0:T(8,128)(2,1)}, f32[512,3072]{1,0:T(8,128)}, bf16[512,3072]{1,0:T(8,128)(2,1)}, f32[512,3072]{1,0:T(8,128)}, f32[512,3072]{1,0:T(8,128)}) fusion(f32[3072]{0:T(1024)S(1)} %bitcast.509, f32[512,3072]{1,0:T(8,128)S(1)} %fusion.183, bf16[768,3072]{1,0:T(8,128)(2,1)S(1)} %copy-done.86, ...), kind=kOutput, calls=%fused_computation.163 | convolution fusion | flops 2625503232 | bytes 37771264 | tf_op jit(solution)/shard_map/dot_general | solution.py:214
  332.6 30.6 %all-gather.26.cloned.1.call-done = bf16[3072,768]{1,0:T(8,128)(2,1)} async-done(((bf16[768,768]{1,0:T(8,128)(2,1)}), bf16[3072,768]{1,0:T(8,128)(2,1)}) %all-gather.26.cloned.1.call-update) | async-done | bytes 4718608 | tf_op jit(solution)/shard_map/all_gather | solution.py:131
  398.0 114.8 %while.66 = (s32[]{:T(128)}, bf16[6,512,2,64]{1,3,2,0:T(8,128)(2,1)}, bf16[6,1024,2,64]{1,3,2,0:T(8,128)(2,1)}, bf16[6,1024,2,64]{1,3,2,0:T(8,128)(2,1)}, bf16[6...) while((s32[]{:T(128)}, ...), condition=%wide.region_23.24_spmd, body=%wide.region_20.23_spmd.sunk | while | flops 682296640 | bytes 39355904 | solution.py:302
  520.9 114.7 %while.67 = (s32[]{:T(128)}, bf16[6,512,2,64]{1,3,2,0:T(8,128)(2,1)}, bf16[6,1024,2,64]{1,3,2,0:T(8,128)(2,1)}, bf16[6,1024,2,64]{1,3,2,0:T(8,128)(2,1)}, bf16[6...) while((s32[]{:T(128)}, ...), condition=%wide.region_33.34_spmd, body=%wide.region_30.33_spmd.sunk | while | flops 682296640 | bytes 39355904 | solution.py:302
  662.3 9.6 reduce-scatter.21.cloned.1.call-done
  714.8 16.7 %reduce-scatter.39.cloned.1.call-done = bf16[192,768]{1,0:T(8,128)(2,1)} async-done(((bf16[768,768]{1,0:T(8,128)(2,1)}), bf16[192,768]{1,0:T(8,128)(2,1)}) %reduce-scatter.39.cloned.1.call-update) | async-done | bytes 294928 | tf_op jit(solution)/shard_map/reduce_scatter | solution.py:383
  733.3 28.3 %reduce-scatter.25.cloned.1.call-done = bf16[192,768]{1,0:T(8,128)(2,1)} async-done(((bf16[768,768]{1,0:T(8,128)(2,1)}), bf16[192,768]{1,0:T(8,128)(2,1)}) %reduce-scatter.25.cloned.1.call-update) | async-done | bytes 294928 | tf_op jit(solution)/shard_map/reduce_scatter | solution.py:368
  761.6 30.1 %reduce-scatter.27.cloned.1.call-done = bf16[192,768]{1,0:T(8,128)(2,1)} async-done(((bf16[768,768]{1,0:T(8,128)(2,1)}), bf16[192,768]{1,0:T(8,128)(2,1)}) %reduce-scatter.27.cloned.1.call-update) | async-done | bytes 294928 | tf_op jit(solution)/shard_map/reduce_scatter | solution.py:368
  803.6 16.9 %all-reduce.28 = (bf16[768]{0:T(1024)(128)(2,1)S(1)}, bf16[768]{0:T(1024)(128)(2,1)S(1)}, bf16[768]{0:T(1024)(128)(2,1)S(1)}, bf16[768]{0:T(1024)(128)(2,1)S(1)}...) all-reduce(bf16[768]{0:T(1024)(128)(2,1)S(1)} %dynamic-update-slice, ...), channel_id=1, replica_groups=mesh['rep'=4,'fsdp'=4,'seq'=2] {'fsdp'}, use_global_device_ids=true, to_apply=%add.7 | all-reduce | flops 19200 | bytes 76800
  821.2 14.9 %all-reduce.26 = (bf16[192]{0:T(256)(128)(2,1)S(1)}, bf16[192]{0:T(256)(128)(2,1)S(1)}, bf16[192]{0:T(256)(128)(2,1)S(1)}, bf16[192]{0:T(256)(128)(2,1)S(1)}, bf...) all-reduce(bf16[192]{0:T(256)(128)(2,1)S(1)} %add_convert_fusion.26, ...), channel_id=1, replica_groups=mesh['rep'=4,'fsdp'=4,'seq'=2] {'rep','seq'}, use_global_device_ids=true, to_apply=%region_42.43 | all-reduce | flops 2304 | bytes 9216 | tf_op jit(solution)/shard_map/psum | solution.py:410
  855.6 28.4 %reduce-scatter.29.cloned.1.call-done = bf16[192,768]{1,0:T(8,128)(2,1)} async-done(((bf16[768,768]{1,0:T(8,128)(2,1)}), bf16[192,768]{1,0:T(8,128)(2,1)}) %reduce-scatter.29.cloned.1.call-update) | async-done | bytes 294928 | tf_op jit(solution)/shard_map/reduce_scatter | solution.py:374
  884.0 30.8 %reduce-scatter.31.cloned.1.call-done = bf16[192,768]{1,0:T(8,128)(2,1)} async-done(((bf16[768,768]{1,0:T(8,128)(2,1)}), bf16[192,768]{1,0:T(8,128)(2,1)}) %reduce-scatter.31.cloned.1.call-update) | async-done | bytes 294928 | tf_op jit(solution)/shard_map/reduce_scatter | solution.py:374
  916.7 86.4 %reduce-scatter.41.cloned.1.call-done = bf16[192,3072]{1,0:T(8,128)(2,1)} async-done(((bf16[768,3072]{1,0:T(8,128)(2,1)}), bf16[192,3072]{1,0:T(8,128)(2,1)}) %reduce-scatter.41.cloned.1.call-update) | async-done | bytes 1179664 | tf_op jit(solution)/shard_map/reduce_scatter | solution.py:395
  1003.1 88.0 %reduce-scatter.43.cloned.1.call-done = bf16[192,3072]{1,0:T(8,128)(2,1)} async-done(((bf16[768,3072]{1,0:T(8,128)(2,1)}), bf16[192,3072]{1,0:T(8,128)(2,1)}) %reduce-scatter.43.cloned.1.call-update) | async-done | bytes 1179664 | tf_op jit(solution)/shard_map/reduce_scatter | solution.py:395
  1094.1 85.1 %reduce-scatter.45.cloned.1.call-done = bf16[768,768]{1,0:T(8,128)(2,1)} async-done(((bf16[3072,768]{1,0:T(8,128)(2,1)}), bf16[768,768]{1,0:T(8,128)(2,1)}) %reduce-scatter.45.cloned.1.call-update) | async-done | bytes 1179664 | tf_op jit(solution)/shard_map/reduce_scatter | solution.py:401
  1179.2 88.0 %reduce-scatter.47.cloned.1.call-done = bf16[768,768]{1,0:T(8,128)(2,1)} async-done(((bf16[3072,768]{1,0:T(8,128)(2,1)}), bf16[768,768]{1,0:T(8,128)(2,1)}) %reduce-scatter.47.cloned.1.call-update) | async-done | bytes 1179664 | tf_op jit(solution)/shard_map/reduce_scatter | solution.py:401
  1284.3 62.8 %all-reduce.32.cloned.1.call-done = (bf16[192,768]{1,0:T(8,128)(2,1)}, bf16[192,768]{1,0:T(8,128)(2,1)}, bf16[192,768]{1,0:T(8,128)(2,1)}, bf16[192,768]{1,0:T(8...) async-done(((bf16[192,768]{1,0:T(8,128)(2,1)}, bf16[192,768]{1,0:T(8,128)(2,1)}, bf16[192,768]{1,0:T(8,128)(2,1)}, bf16[192,768]{1,0:T(8,128)(2,1)}, ...) | async-done | bytes 3538960 | tf_op jit(solution)/shard_map/psum | solution.py:410
  (806 shorter events, 619.4 us)
Async XLA Ops:
  7.9 62.7 %all-gather.20.cloned.1.call-start = ((), (), s32[]{:S(2)}) async-start(), calls=%async_computation.18 | async-start | bytes 1474560 | tf_op jit(solution)/shard_map/all_gather | solution.py:122
  8.7 93.3 %all-gather.18.cloned.1.call-start = ((), (), s32[]{:S(2)}) async-start(), calls=%async_computation.17 | async-start | bytes 1474560 | tf_op jit(solution)/shard_map/all_gather | solution.py:120
  9.4 106.1 %all-gather.28.cloned.1.call-start = ((), (), s32[]{:S(2)}) async-start(), calls=%async_computation.38 | async-start | bytes 2359296 | tf_op jit(solution)/shard_map/all_gather | solution.py:169
  42.7 85.2 %all-gather.30.cloned.1.call-start = ((), (), s32[]{:S(2)}) async-start(), calls=%async_computation.39 | async-start | bytes 2359296 | tf_op jit(solution)/shard_map/all_gather | solution.py:166
  73.8 130.2 %all-gather.22.cloned.1.call-start = ((), (), s32[]{:S(2)}) async-start(), calls=%async_computation.19 | async-start | bytes 1474560 | tf_op jit(solution)/shard_map/all_gather | solution.py:125
  74.4 133.9 %all-gather.32.cloned.1.call-start = ((), (), s32[]{:S(2)}) async-start(), calls=%async_computation.40 | async-start | bytes 2359296 | tf_op jit(solution)/shard_map/all_gather | solution.py:169
  76.3 134.6 %all-gather.34.cloned.1.call-start = ((), (), s32[]{:S(2)}) async-start(), calls=%async_computation.41 | async-start | bytes 2359296 | tf_op jit(solution)/shard_map/all_gather | solution.py:166
  79.4 210.7 %all-gather.24.cloned.1.call-start = ((), (), s32[]{:S(2)}) async-start(), calls=%async_computation.20 | async-start | bytes 5898240 | tf_op jit(solution)/shard_map/all_gather | solution.py:129
  80.2 283.0 %all-gather.26.cloned.1.call-start = ((), (), s32[]{:S(2)}) async-start(), calls=%async_computation.21 | async-start | bytes 5898240 | tf_op jit(solution)/shard_map/all_gather | solution.py:131
  80.8 565.9 %reduce-scatter.19.cloned.1.call-start = ((), (), s32[]{:S(2)}) async-start(), calls=%async_computation.23 | async-start | bytes 2359296 | tf_op jit(solution)/shard_map/reduce_scatter | solution.py:313
  512.8 137.2 %reduce-scatter.23.cloned.1.call-start = ((), (), s32[]{:S(2)}) async-start(), calls=%async_computation.25 | async-start | bytes 2359296 | tf_op jit(solution)/shard_map/reduce_scatter | solution.py:313
  636.9 77.8 %reduce-scatter.37.cloned.1.call-start = ((), (), s32[]{:S(2)}) async-start(), calls=%async_computation.32 | async-start | bytes 1474560 | tf_op jit(solution)/shard_map/reduce_scatter | solution.py:383
  638.9 92.6 %reduce-scatter.39.cloned.1.call-start = ((), (), s32[]{:S(2)}) async-start(), calls=%async_computation.33 | async-start | bytes 1474560 | tf_op jit(solution)/shard_map/reduce_scatter | solution.py:383
  642.1 119.5 %reduce-scatter.25.cloned.1.call-start = ((), (), s32[]{:S(2)}) async-start(), calls=%async_computation.26 | async-start | bytes 1474560 | tf_op jit(solution)/shard_map/reduce_scatter | solution.py:368
  644.3 147.4 %reduce-scatter.27.cloned.1.call-start = ((), (), s32[]{:S(2)}) async-start(), calls=%async_computation.27 | async-start | bytes 1474560 | tf_op jit(solution)/shard_map/reduce_scatter | solution.py:368
  646.5 199.6 %reduce-scatter.33.cloned.1.call-start = ((), (), s32[]{:S(2)}) async-start(), calls=%async_computation.30 | async-start | bytes 1474560 | tf_op jit(solution)/shard_map/reduce_scatter | solution.py:377
  649.9 203.8 %reduce-scatter.35.cloned.1.call-start = ((), (), s32[]{:S(2)}) async-start(), calls=%async_computation.31 | async-start | bytes 1474560 | tf_op jit(solution)/shard_map/reduce_scatter | solution.py:377
  653.3 230.8 %reduce-scatter.29.cloned.1.call-start = ((), (), s32[]{:S(2)}) async-start(), calls=%async_computation.28 | async-start | bytes 1474560 | tf_op jit(solution)/shard_map/reduce_scatter | solution.py:374
  662.2 252.7 %reduce-scatter.31.cloned.1.call-start = ((), (), s32[]{:S(2)}) async-start(), calls=%async_computation.29 | async-start | bytes 1474560 | tf_op jit(solution)/shard_map/reduce_scatter | solution.py:374
  675.1 328.0 %reduce-scatter.41.cloned.1.call-start = ((), (), s32[]{:S(2)}) async-start(), calls=%async_computation.34 | async-start | bytes 5898240 | tf_op jit(solution)/shard_map/reduce_scatter | solution.py:395
  681.7 409.4 %reduce-scatter.43.cloned.1.call-start = ((), (), s32[]{:S(2)}) async-start(), calls=%async_computation.35 | async-start | bytes 5898240 | tf_op jit(solution)/shard_map/reduce_scatter | solution.py:395
  689.6 489.6 %reduce-scatter.45.cloned.1.call-start = ((), (), s32[]{:S(2)}) async-start(), calls=%async_computation.36 | async-start | bytes 5898240 | tf_op jit(solution)/shard_map/reduce_scatter | solution.py:401
  697.8 569.4 %reduce-scatter.47.cloned.1.call-start = ((), (), s32[]{:S(2)}) async-start(), calls=%async_computation.37 | async-start | bytes 5898240 | tf_op jit(solution)/shard_map/reduce_scatter | solution.py:401
  704.6 642.5 %all-reduce.32.cloned.1.call-start = ((), (), s32[]{:S(2)}) async-start(), calls=%async_computation.42 | async-start | bytes 7077888 | tf_op jit(solution)/shard_map/psum | solution.py:410
  (100 other events, 1345.8 us)
Sparse Core Ops, SparseCore 0:
  9.6 29.9 all-gather.15
  41.2 29.4 all-gather.19
  72.3 29.6 all-gather.17
  103.9 11.5 all-gather.27
  116.9 10.9 all-gather.29
  129.3 28.9 all-gather.21
  160.4 11.5 all-gather.31
  174.1 11.0 all-gather.33
  186.7 87.1 all-gather.23
  275.4 87.7 all-gather.25
  512.9 10.6 reduce-scatter.18
  674.0 27.2 reduce-scatter.36
  703.5 27.9 reduce-scatter.38
  733.6 27.9 reduce-scatter.24
  763.8 27.9 reduce-scatter.26
  794.0 29.3 reduce-scatter.32
  825.6 28.0 reduce-scatter.34
  856.1 27.9 reduce-scatter.28
  886.9 27.9 reduce-scatter.30
  917.2 85.8 reduce-scatter.40
  1005.3 85.7 reduce-scatter.42
  1093.4 85.7 reduce-scatter.44
  1181.4 85.7 reduce-scatter.46
  1272.3 74.7 all-reduce.31
  (3 shorter events, 30.9 us)
where the time goes:
time: 1370 us; the launch traced here: 1360 us
  waiting for transfers between devices  665 us (49%)
  matrix products  353 us (26%)
  local copies, waits for them, and re-layouts  192 us (14%)
  other arithmetic  75.3 us (5%)
  blocking collectives  55.9 us (4%)
  between operations  17.9 us (1%)
    reduce_scatter x2, waiting for transfers between devices, on_device(): lax.psum_scatter(grad_list[11].astype(jnp.bfloat16), 'fsdp', scatter_dime...  174 us
    reduce_scatter x2, waiting for transfers between devices, on_device(): lax.psum_scatter(grad_list[13].astype(jnp.bfloat16), 'fsdp', scatter_dime...  173 us
    reshape x24, local copies, waits for them, and re-layouts, token_allowed(): expanded.reshape(head_count, count_rows, block_total * block_size)  113 us
    psum x1, waiting for transfers between devices, on_device(): lax.psum(as_sent(collected), ('rep', 'seq'))  62.8 us
    reduce_scatter x2, waiting for transfers between devices, on_device(): lax.psum_scatter(grad_list[4].astype(jnp.bfloat16), 'fsdp', scatter_dimen...  59.3 us
    reduce_scatter x2, waiting for transfers between devices, on_device(): lax.psum_scatter(grad_list[2].astype(jnp.bfloat16), 'fsdp', scatter_dimen...  58.4 us
    dot_general x2, matrix products, on_device(): jnp.dot(normed_two, w_up, preferred_element_type=jnp.float32)  39.8 us
    dot_general x12, matrix products, backward_pair(): jnp.einsum('qhd,khd->hqk', query_part, key_part, preferred_element_type=j...  35.3 us
  transfers between devices with their start and end apart: 27, of which 19 were waited for; matrix products, arithmetic and copies ran while one was open for 33% of the time, Pallas kernels for 0%

commit v1 on v0

v1 whole, which is shorter than its diff:
```python
import functools
import jax
import jax.numpy as jnp
from jax import lax
from jax.experimental import pallas as pl
from jax.experimental.pallas import tpu as pltpu
from jax.sharding import PartitionSpec as P

norm_eps = 1e-05

HEADS = 12
HDIM = 64
BLOCK = 64
TQ = 256
TK = 256
NEG = -1e30


def nt(a, b):
    return lax.dot_general(a, b, (((1,), (1,)), ((), ())), preferred_element_type=jnp.float32)


def tn(a, b):
    return lax.dot_general(a, b, (((0,), (0,)), ((), ())), preferred_element_type=jnp.float32)


def nn(a, b):
    return jnp.dot(a, b, preferred_element_type=jnp.float32)


def head_lanes(head):
    lane = lax.broadcasted_iota(jnp.int32, (1, 128), 1)
    return (lane < HDIM) if head == 0 else (lane >= HDIM)


def bias_rows(block_ref, doc_ref, head, tile):
    per = TQ // BLOCK
    rows = [
        jnp.broadcast_to(
            block_ref[0, head, pl.ds(tile * per + b, 1), :], (BLOCK, 128)
        )
        for b in range(per)
    ]
    return (jnp.concatenate(rows, axis=0) + doc_ref[0, pl.ds(tile * TQ, TQ), :]).astype(jnp.bfloat16)


def forward_body(
    span_ref, q_ref, ko_ref, vo_ref, kx_ref, vx_ref, ao_ref, ax_ref, block_ref, doc_ref,
    out_ref, lse_ref, acc_ref, qa_ref,
):
    micro = pl.program_id(0)
    tiles = q_ref.shape[1] // TQ
    group = q_ref.shape[2] // HDIM
    for tile in range(tiles):
        for head in range(group):
            cols = pl.ds(head // 2 * 128, 128)
            q_rows = q_ref[0, pl.ds(tile * TQ, TQ), cols].astype(jnp.float32) * 0.125
            masked = jnp.where(head_lanes(head % 2), q_rows, 0.0).astype(jnp.bfloat16)
            qa_ref[head, :, 0:128] = masked
            qa_ref[head, :, 128:256] = bias_rows(block_ref, doc_ref, head, tile)
        acc_ref[...] = jnp.zeros_like(acc_ref)

        def sweep(k_ref, v_ref, a_ref, base, state):
            def step(j, carry):
                at = pl.ds(pl.multiple_of(j * TK, TK), TK)
                aug = a_ref[0, at, :]
                scores = []
                for head in range(group):
                    cols = pl.ds(head // 2 * 128, 128)
                    k_aug = jnp.concatenate([k_ref[0, at, cols], aug], axis=1)
                    scores.append(nt(k_aug, qa_ref[head]))
                fresh = []
                probs = []
                for head in range(group):
                    top_new = jnp.maximum(carry[head], jnp.max(scores[head], axis=0, keepdims=True))
                    probs.append(jnp.exp(scores[head] - top_new).astype(jnp.bfloat16))
                    fresh.append(top_new)
                for head in range(group):
                    cols = pl.ds(head // 2 * 128, 128)
                    v_rows = jnp.where(head_lanes(head % 2), v_ref[0, at, cols], jnp.bfloat16(1.0))
                    part = tn(v_rows, probs[head])
                    acc_ref[head] = acc_ref[head] * jnp.exp(carry[head] - fresh[head]) + part
                return tuple(fresh)

            return lax.fori_loop(span_ref[micro, tile, base], span_ref[micro, tile, base + 1], step, state)

        state = tuple(jnp.full((1, TQ), -3e38, jnp.float32) for _ in range(group))
        state = sweep(ko_ref, vo_ref, ao_ref, 0, state)
        state = sweep(kx_ref, vx_ref, ax_ref, 2, state)
        for pair in range(group // 2):
            done = []
            for head in range(2):
                at = pair * 2 + head
                mass = acc_ref[at, pl.ds((1 - head) * HDIM, 1), :]
                done.append(acc_ref[at, pl.ds(head * HDIM, HDIM), :] / mass)
                lse_ref[0, pair, pl.ds(head, 1), pl.ds(tile * TQ, TQ)] = state[at] + jnp.log(mass)
            out_ref[0, pl.ds(tile * TQ, TQ), pl.ds(pair * 128, 128)] = (
                jnp.concatenate(done, axis=0).T.astype(out_ref.dtype)
            )


def backward_body(
    span_ref, q_ref, ko_ref, vo_ref, kx_ref, vx_ref, ao_ref, ax_ref, block_ref, doc_ref,
    mixed_ref, grad_ref, lse_ref,
    dq_ref, dko_ref, dvo_ref, dkx_ref, dvx_ref,
    dqt_ref, qa_ref, gm_ref, ko_acc, vo_acc, kx_acc, vx_acc,
):
    micro = pl.program_id(0)
    tiles = q_ref.shape[1] // TQ
    group = q_ref.shape[2] // HDIM
    for ref in (ko_acc, vo_acc, kx_acc, vx_acc):
        ref[...] = jnp.zeros_like(ref)
    for tile in range(tiles):
        rows = pl.ds(tile * TQ, TQ)
        inner = []
        for pair in range(group // 2):
            cols = pl.ds(pair * 128, 128)
            q_rows = q_ref[0, rows, cols].astype(jnp.float32) * 0.125
            grad_rows = grad_ref[0, rows, cols].astype(jnp.float32)
            both = (mixed_ref[0, rows, cols].astype(jnp.float32) * grad_rows).T
            for side in range(2):
                head = pair * 2 + side
                qa_ref[head, :, 0:128] = jnp.where(head_lanes(side), q_rows, 0.0).astype(jnp.bfloat16)
                qa_ref[head, :, 128:256] = bias_rows(block_ref, doc_ref, head, tile)
                gm_ref[head] = jnp.where(head_lanes(side), grad_rows, 0.0).astype(jnp.bfloat16)
                inner.append(jnp.sum(both[side * HDIM:(side + 1) * HDIM, :], axis=0, keepdims=True))
        dqt_ref[...] = jnp.zeros_like(dqt_ref)

        def sweep(k_ref, v_ref, a_ref, k_acc, v_acc, base):
            def step(j, carry):
                at = pl.ds(pl.multiple_of(j * TK, TK), TK)
                aug = a_ref[0, at, :]
                for chunk in range(0, group, CHUNK):
                    heads = range(chunk, min(chunk + CHUNK, group))
                    scores, grads, probs, souls = {}, {}, {}, {}
                    for head in heads:
                        cols = pl.ds(head // 2 * 128, 128)
                        k_aug = jnp.concatenate([k_ref[0, at, cols], aug], axis=1)
                        scores[head] = nt(k_aug, qa_ref[head])
                        grads[head] = nt(v_ref[0, at, cols], gm_ref[head])
                    for head in heads:
                        weight = jnp.exp(scores[head] - lse_ref[0, head // 2, pl.ds(head % 2, 1), rows])
                        souls[head] = (weight * (grads[head] - carry[head])).astype(jnp.bfloat16)
                        probs[head] = weight.astype(jnp.bfloat16)
                    for head in heads:
                        cols = pl.ds(head // 2 * 128, 128)
                        dv = nn(probs[head], gm_ref[head])
                        dk = nn(souls[head], qa_ref[head, :, 0:128])
                        dqt = tn(k_ref[0, at, cols], souls[head])
                        lanes = pl.ds(head * HDIM, HDIM)
                        side = head % 2
                        dqt_ref[lanes, :] += dqt[side * HDIM:(side + 1) * HDIM, :]
                        if side == 0:
                            dv_low, dk_low = dv, dk
                        else:
                            k_acc[at, cols] += dk + dk_low
                            v_acc[at, cols] += dv + dv_low
                return carry

            lax.fori_loop(span_ref[micro, tile, base], span_ref[micro, tile, base + 1], step, tuple(inner))

        sweep(ko_ref, vo_ref, ao_ref, ko_acc, vo_acc, 0)
        sweep(kx_ref, vx_ref, ax_ref, kx_acc, vx_acc, 2)
        for pair in range(group // 2):
            cols = pl.ds(pair * 128, 128)
            dq_ref[0, rows, cols] = (dqt_ref[cols, :] * 0.125).T.astype(dq_ref.dtype)
    dko_ref[0] = ko_acc[...].astype(dko_ref.dtype)
    dvo_ref[0] = vo_acc[...].astype(dvo_ref.dtype)
    dkx_ref[0] = kx_acc[...].astype(dkx_ref.dtype)
    dvx_ref[0] = vx_acc[...].astype(dvx_ref.dtype)


CHUNK = 4


def specs(half, group):
    pair = pl.BlockSpec((1, half, group * HDIM), lambda m, p, s: (m, 0, p))
    aug = pl.BlockSpec((1, half, 128), lambda m, p, s: (m, 0, 0))
    block = pl.BlockSpec((1, group, half // BLOCK, 128), lambda m, p, s: (m, p, 0, 0))
    lse = pl.BlockSpec((1, group // 2, 2, half), lambda m, p, s: (m, p, 0, 0))
    return pair, aug, block, lse


def attend_forward(span, q, ko, vo, kx, vx, ao, ax, block, doc, group=12):
    micro, half, width = q.shape
    pairs = group // 2
    pair = pl.BlockSpec((1, half, group * HDIM), lambda m, p, s: (m, 0, p))
    aug = pl.BlockSpec((1, half, 128), lambda m, p, s: (m, 0, 0))
    blk = pl.BlockSpec((1, group, half // BLOCK, 128), lambda m, p, s: (m, p, 0, 0))
    lse = pl.BlockSpec((1, pairs, 2, half), lambda m, p, s: (m, p, 0, 0))
    return pl.pallas_call(
        forward_body,
        name="attend_forward",
        out_shape=(
            jax.ShapeDtypeStruct((micro, half, width), jnp.bfloat16),
            jax.ShapeDtypeStruct((micro, HEADS // 2, 2, half), jnp.float32),
        ),
        grid_spec=pltpu.PrefetchScalarGridSpec(
            num_scalar_prefetch=1,
            grid=(micro, HEADS // group),
            in_specs=[pair] * 5 + [aug, aug, blk, aug],
            out_specs=(pair, lse),
            scratch_shapes=[
                pltpu.VMEM((group, 128, TQ), jnp.float32),
                pltpu.VMEM((group, TQ, 256), jnp.bfloat16),
            ],
        ),
        cost_estimate=pl.CostEstimate(flops=20_000_000_000, bytes_accessed=20_000_000, transcendentals=0),
    )(span, q, ko, vo, kx, vx, ao, ax, block, doc)


def attend_backward(span, q, ko, vo, kx, vx, ao, ax, block, doc, mixed, grad, lse, group=12):
    micro, half, width = q.shape
    pair, aug, blk, lse_spec = specs(half, group)
    shape = jax.ShapeDtypeStruct((micro, half, width), jnp.bfloat16)
    return pl.pallas_call(
        backward_body,
        name="attend_backward",
        out_shape=(shape,) * 5,
        grid_spec=pltpu.PrefetchScalarGridSpec(
            num_scalar_prefetch=1,
            grid=(micro, HEADS // group),
            in_specs=[pair] * 5 + [aug, aug, blk, aug, pair, pair, lse_spec],
            out_specs=(pair,) * 5,
            scratch_shapes=[
                pltpu.VMEM((group * HDIM, TQ), jnp.float32),
                pltpu.VMEM((group, TQ, 256), jnp.bfloat16),
                pltpu.VMEM((group, TQ, 128), jnp.bfloat16),
            ]
            + [pltpu.VMEM((half, group * HDIM), jnp.float32)] * 4,
        ),
        cost_estimate=pl.CostEstimate(flops=40_000_000_000, bytes_accessed=40_000_000, transcendentals=0),
    )(span, q, ko, vo, kx, vx, ao, ax, block, doc, mixed, grad, lse)


def tables(segment, rand_blocks, side, half):
    micro, length = segment.shape
    blocks = length // BLOCK
    mine = half // BLOCK
    lane = lax.broadcasted_iota(jnp.int32, (1, 1, 128), 2)
    own = lax.dynamic_slice_in_dim(segment, side * half, half, axis=1)
    other = lax.dynamic_slice_in_dim(segment, (1 - side) * half, half, axis=1)

    def aug(seg, which):
        place = (which * half + lax.broadcasted_iota(jnp.int32, (1, half, 1), 1)) // BLOCK
        hit = (lane == place) | (lane == seg[:, :, None] + blocks)
        return hit.astype(jnp.bfloat16)

    doc = jnp.where((lane >= blocks) & (lane < blocks + 4) & (lane != own[:, :, None] + blocks), NEG, 0.0)
    q_block = side * mine + lax.broadcasted_iota(jnp.int32, (1, 1, mine, 1), 2)
    k_block = lax.broadcasted_iota(jnp.int32, (1, 1, 1, 128), 3)
    chosen = lax.dynamic_slice_in_dim(rand_blocks, side * mine, mine, axis=2)
    allowed = (jnp.abs(q_block - k_block) <= 1) | (k_block == 0) | (k_block == blocks - 1)
    allowed = allowed | (q_block == 0) | (q_block == blocks - 1) | (k_block >= blocks)
    for pick in range(rand_blocks.shape[3]):
        allowed = allowed | (chosen[:, :, :, pick:pick + 1] == k_block)
    block = jnp.where(allowed, 0.0, NEG).astype(jnp.float32)
    tiles = half // TQ
    first = own.reshape(micro, tiles, TQ)[:, :, 0]
    last = own.reshape(micro, tiles, TQ)[:, :, TQ - 1]
    begin = jnp.sum((segment[:, None, :] < first[:, :, None]).astype(jnp.int32), axis=-1)
    end = jnp.sum((segment[:, None, :] <= last[:, :, None]).astype(jnp.int32), axis=-1)
    span = []
    for base in (side * half, (1 - side) * half):
        low = jnp.clip((begin - base) // TK, 0, half // TK)
        high = jnp.clip((end - base + TK - 1) // TK, 0, half // TK)
        span += [low, jnp.maximum(high, low)]
    return jnp.stack(span, axis=-1), aug(own, side), aug(other, 1 - side), block, doc.astype(jnp.float32)


MESH = pl.DeviceIdType.MESH
GROUPS = 3


def place():
    rep, shard, side = lax.axis_index("rep"), lax.axis_index("fsdp"), lax.axis_index("seq")
    quad = lax.rem(rep, 4)
    across, along = lax.rem(quad, 2), quad // 2
    near = (1 - 2 * across, 2 - 4 * along)
    return rep, shard, side, quad, near


def chunk(refs, group, shard, quad, side, rows, half=None):
    width = 768 if half is None else 384
    offset = 0 if half is None else half * 384
    low = side * rows
    if group == 0:
        return refs[0].at[quad, pl.ds(pl.multiple_of(shard * (2 * rows) + low, 16), rows), pl.ds(offset, width)]
    if group == 1:
        at = pl.multiple_of(shard * (2 * rows) + low, 16)
        return refs[1].at[pl.ds(at, rows), pl.ds(pl.multiple_of(quad * 768 + offset, 128), width)]
    at = pl.multiple_of(shard * (8 * rows) + quad * (2 * rows) + low, 16)
    return refs[2].at[pl.ds(at, rows), pl.ds(offset, width)]


def greet(peers):
    barrier = pltpu.get_barrier_semaphore()
    for peer in peers:
        pl.semaphore_signal(barrier, inc=1, device_id=peer, device_id_type=MESH)
    pl.semaphore_wait(barrier, len(peers))


def remote(src, dst, send, recv, peer):
    return pltpu.make_async_remote_copy(
        src_ref=src, dst_ref=dst, send_sem=send, recv_sem=recv, device_id=peer, device_id_type=MESH
    )


def gather_body(
    shards, rows, qkvo_in, up_in, down_in, vec_in, qkvo_out, up_out, down_out, vec_out,
    qkvo_stage, up_stage, down_stage, vec_stage,
    in_sem, out_sem, z_send, z_recv, x_send, x_recv, y_send, y_recv, d_send, d_recv, c_send, c_recv,
):
    rep, shard, side, quad, (dx, dy) = place()
    ins, outs = (qkvo_in, up_in, down_in), (qkvo_out, up_out, down_out)
    stages = (qkvo_stage, up_stage, down_stage, vec_stage)
    x_peer, y_peer, partner = (rep + dx, shard, side), (rep + dy, shard, side), (rep, shard, 1 - side)
    z_peers = [(rep, lax.rem(shard + k, shards), side) for k in range(1, shards)]
    for i, src in enumerate((qkvo_in, up_in, down_in, vec_in)):
        pltpu.make_async_copy(src, stages[i], in_sem.at[i]).start()
    greet(z_peers + [x_peer, y_peer, partner])
    sent = []

    def go(copy):
        copy.start()
        sent.append(copy)

    for g in range(GROUPS):
        for k in range(1, shards):
            go(remote(
                chunk(ins, g, 0, quad, side, rows), chunk(outs, g, shard, quad, side, rows),
                z_send.at[g, k - 1], z_recv.at[g, shards - k - 1], z_peers[k - 1],
            ))
        if g == 0:
            for k in range(1, shards):
                go(remote(
                    vec_in, vec_out.at[shard],
                    z_send.at[GROUPS, k - 1], z_recv.at[GROUPS, shards - k - 1], z_peers[k - 1],
                ))
    owned = (
        qkvo_out.at[:, pl.ds(pl.multiple_of(shard * 2 * rows, 16), 2 * rows), :],
        up_out.at[pl.ds(pl.multiple_of(shard * 2 * rows, 16), 2 * rows), :],
        down_out.at[pl.ds(pl.multiple_of(shard * 8 * rows, 16), 8 * rows), :],
        vec_out.at[shard],
    )
    local = []
    for i, src in enumerate((qkvo_in, up_in, down_in, vec_in)):
        pltpu.make_async_copy(src, stages[i], in_sem.at[i]).wait()
        copy = pltpu.make_async_copy(stages[i], owned[i], out_sem.at[i])
        copy.start()
        local.append(copy)

    def piece(g, k, member, core, half=None):
        return chunk(outs, g, lax.rem(shard + k, shards), member, core, rows, half)

    def hop(g, k, member, core, send, recv, peer, half=None):
        ref = piece(g, k, member, core, half)
        return remote(ref, ref, send, recv, peer)

    x_quad, y_quad, d_quad = quad + dx, quad + dy, quad + dx + dy

    def straight(g):
        for k in range(1, shards):
            hop(g, k, quad, side, z_send.at[g, k - 1], z_recv.at[g, k - 1], z_peers[k - 1]).wait_recv()
            go(hop(g, k, quad, side, x_send.at[g, k - 1], x_recv.at[g, k - 1], x_peer))
            go(hop(g, k, quad, side, y_send.at[g, k - 1], y_recv.at[g, k - 1], y_peer))
            go(hop(g, k, quad, side, c_send.at[g, k - 1, 0], c_recv.at[g, k - 1, 0], partner))

    def turn(g):
        for k in range(1, shards):
            hop(g, k, x_quad, side, x_send.at[g, k - 1], x_recv.at[g, k - 1], x_peer).wait_recv()
            go(hop(g, k, x_quad, side, d_send.at[g, k - 1, 1], d_recv.at[g, k - 1, 1], y_peer, 1))
            go(hop(g, k, x_quad, side, c_send.at[g, k - 1, 1], c_recv.at[g, k - 1, 1], partner))
            hop(g, k, y_quad, side, y_send.at[g, k - 1], y_recv.at[g, k - 1], y_peer).wait_recv()
            go(hop(g, k, y_quad, side, d_send.at[g, k - 1, 0], d_recv.at[g, k - 1, 0], x_peer, 0))
            go(hop(g, k, y_quad, side, c_send.at[g, k - 1, 2], c_recv.at[g, k - 1, 2], partner))

    def corner(g):
        for k in range(1, shards):
            hop(g, k, d_quad, side, d_send.at[g, k - 1, 0], d_recv.at[g, k - 1, 0], x_peer, 0).wait_recv()
            hop(g, k, d_quad, side, d_send.at[g, k - 1, 1], d_recv.at[g, k - 1, 1], y_peer, 1).wait_recv()
            go(hop(g, k, d_quad, side, c_send.at[g, k - 1, 3], c_recv.at[g, k - 1, 3], partner))

    straight(0)
    for g in range(GROUPS):
        turn(g)
        if g + 1 < GROUPS:
            straight(g + 1)
        corner(g)
    for g in range(GROUPS):
        for k in range(1, shards):
            for i, member in enumerate((quad, x_quad, y_quad, d_quad)):
                hop(g, k, member, 1 - side, c_send.at[g, k - 1, i], c_recv.at[g, k - 1, i], partner).wait_recv()
    for k in range(1, shards):
        remote(
            vec_in, vec_out.at[lax.rem(shard + k, shards)],
            z_send.at[GROUPS, k - 1], z_recv.at[GROUPS, k - 1], z_peers[k - 1],
        ).wait_recv()
    for copy in sent:
        copy.wait_send()
    for copy in local:
        copy.wait()


def gather_weights(shards, qkvo, up, down, vec):
    rows = qkvo.shape[1] // 2
    model = qkvo.shape[2]
    hidden = up.shape[1]
    any_space = pl.BlockSpec(memory_space=pl.ANY)
    dma = pltpu.SemaphoreType.DMA
    low = jnp.bfloat16
    return pl.pallas_call(
        functools.partial(gather_body, shards, rows),
        name="gather_weights",
        out_shape=(
            jax.ShapeDtypeStruct((4, model, model), low),
            jax.ShapeDtypeStruct((model, hidden), low),
            jax.ShapeDtypeStruct((hidden, model), low),
            jax.ShapeDtypeStruct((shards,) + vec.shape, low),
        ),
        in_specs=[any_space] * 4,
        out_specs=(any_space,) * 4,
        scratch_shapes=[
            pltpu.VMEM(qkvo.shape, low), pltpu.VMEM(up.shape, low),
            pltpu.VMEM(down.shape, low), pltpu.VMEM(vec.shape, low),
            dma((4,)), dma((4,)),
            dma((GROUPS + 1, shards - 1)), dma((GROUPS + 1, shards - 1)),
        ]
        + [dma((GROUPS, shards - 1))] * 4
        + [dma((GROUPS, shards - 1, 2))] * 2
        + [dma((GROUPS, shards - 1, 4))] * 2,
        compiler_params=pltpu.CompilerParams(collective_id=0, has_side_effects=True),
    )(qkvo, up, down, vec)


def add_into(out_ref, refs):
    total = refs[0][...].astype(jnp.float32)
    for ref in refs[1:]:
        total = total + ref[...].astype(jnp.float32)
    out_ref[...] = total.astype(out_ref.dtype)


def reduce_body(
    shards, quads, rows, qkvo_in, up_in, down_in, vec_in, qkvo_out, up_out, down_out, vec_out,
    own, mate, first, second, last, ring, full, vec_sum, vec_mate, vec_last, vec_ring,
    load_sem, c_send, c_recv, f_send, f_recv, s_send, s_recv, z_send, z_recv, q_send, q_recv,
    x_send, x_recv, y_send, y_recv, d_send, d_recv, g_send, g_recv, out_sem, v_send, v_recv,
):
    rep, shard, side, quad, (dx, dy) = place()
    ins, outs = (qkvo_in, up_in, down_in), (qkvo_out, up_out, down_out)
    x_peer, y_peer, partner = (rep + dx, shard, side), (rep + dy, shard, side), (rep, shard, 1 - side)
    x_quad, y_quad, d_quad = quad + dx, quad + dy, quad + dx + dy
    z_peers = [(rep, lax.rem(shard + k, shards), side) for k in range(1, shards)]
    q_peers = [(lax.rem(rep + 4 * k, 4 * quads), shard, side) for k in range(1, quads)]
    greet(z_peers + q_peers + [x_peer, y_peer, partner])

    def c_copy(g, f, m):
        return remote(chunk(ins, g, f, m, 1 - side, rows), mate.at[g, f, m], c_send.at[g, f, m], c_recv.at[g, f, m], partner)

    def load(g, f, m):
        return pltpu.make_async_copy(chunk(ins, g, f, m, side, rows), own.at[g, f, m], load_sem.at[g, f, m])

    def f_copy(g, f, slot, flip):
        peer, to = (y_peer, y_quad) if flip else (x_peer, x_quad)
        member = to if slot == 0 else d_quad
        return remote(own.at[g, f, member], first.at[g, f, slot], f_send.at[g, f, slot], f_recv.at[g, f, slot], peer)

    def s_copy(g, f, flip):
        peer, to = (x_peer, x_quad) if flip else (y_peer, y_quad)
        return remote(own.at[g, f, to], second.at[g, f], s_send.at[g, f], s_recv.at[g, f], peer)

    vec_copies = []

    def vec_go(src, dst, i, peer):
        copy = remote(src, dst, v_send.at[i], v_recv.at[i], peer)
        copy.start()
        vec_copies.append(copy)
        return copy

    swap = vec_go(vec_in, vec_mate.at[0], 0, partner)
    for g in range(GROUPS):
        def begin(f, carry, g=g):
            for m in range(4):
                c_copy(g, f, m).start()
                load(g, f, m).start()
            return carry
        lax.fori_loop(0, shards, begin, 0)

    def merge(g):
        def step(pairs, carry):
            for flip in range(2):
                f = pairs * 2 + flip
                for m in range(4):
                    load(g, f, m).wait()
                    c_copy(g, f, m).wait_recv()
                    add_into(own.at[g, f, m], (own.at[g, f, m], mate.at[g, f, m]))
                for slot in range(2):
                    f_copy(g, f, slot, flip).start()
            return carry
        lax.fori_loop(0, shards // 2, step, 0)

    def fold(g):
        def step(pairs, carry):
            for flip in range(2):
                f = pairs * 2 + flip
                for slot in range(2):
                    f_copy(g, f, slot, flip).wait()
                    member = quad if slot == 0 else (x_quad if flip else y_quad)
                    add_into(own.at[g, f, member], (own.at[g, f, member], first.at[g, f, slot]))
                s_copy(g, f, flip).start()
            return carry
        lax.fori_loop(0, shards // 2, step, 0)

    def settle(g):
        def step(pairs, carry):
            for flip in range(2):
                f = pairs * 2 + flip
                s_copy(g, f, flip).wait()
                add_into(own.at[g, f, quad], (own.at[g, f, quad], second.at[g, f]))
            return carry
        lax.fori_loop(0, shards // 2, step, 0)
        for k in range(1, shards):
            z_copy(g, k).start()

    def z_copy(g, k):
        return remote(
            own.at[g, lax.rem(shard + k, shards), quad], last.at[g, shards - k - 1],
            z_send.at[g, k - 1], z_recv.at[g, shards - k - 1], z_peers[k - 1],
        )

    def z_wait(g, k):
        remote(own.at[g, shard, quad], last.at[g, k - 1], z_send.at[g, k - 1], z_recv.at[g, k - 1], z_peers[k - 1]).wait_recv()

    merge(0)
    swap.wait_recv()
    vec_sum[...] = vec_in[...] + vec_mate[0]
    swap = vec_go(vec_sum, vec_mate.at[1], 1, x_peer)
    merge(1)
    fold(0)
    swap.wait()
    vec_sum[...] = vec_sum[...] + vec_mate[1]
    swap = vec_go(vec_sum, vec_mate.at[2], 2, y_peer)
    merge(2)
    fold(1)
    settle(0)
    swap.wait()
    vec_sum[...] = vec_sum[...] + vec_mate[2]
    for k in range(1, shards):
        copy = remote(
            vec_sum.at[lax.rem(shard + k, shards)], vec_last.at[shards - k - 1],
            v_send.at[2 + k], v_recv.at[2 + shards - k], z_peers[k - 1],
        )
        copy.start()
    fold(2)
    settle(1)
    settle(2)

    def swirl(g):
        for k in range(1, shards):
            z_wait(g, k)
        add_into(full.at[g, quad, side], [own.at[g, shard, quad]] + [last.at[g, k] for k in range(shards - 1)])
        for k in range(1, quads):
            remote(full.at[g, quad, side], ring.at[g, quads - k - 1], q_send.at[g, k - 1], q_recv.at[g, quads - k - 1], q_peers[k - 1]).start()
        for k in range(1, quads):
            remote(full.at[g, quad, side], ring.at[g, k - 1], q_send.at[g, k - 1], q_recv.at[g, k - 1], q_peers[k - 1]).wait()
        if quads > 1:
            add_into(full.at[g, quad, side], [full.at[g, quad, side]] + [ring.at[g, k] for k in range(quads - 1)])
        spread(g, quad, x_send.at[g], x_recv.at[g], x_peer).start()
        spread(g, quad, y_send.at[g], y_recv.at[g], y_peer).start()
        spread(g, quad, g_send.at[g, 0], g_recv.at[g, 0], partner).start()

    def spread(g, member, send, recv, peer, half=None, core=None):
        core = side if core is None else core
        ref = full.at[g, member, core]
        if half is not None:
            ref = full.at[g, member, core, :, pl.ds(half * 384, 384)]
        return remote(ref, ref, send, recv, peer)

    def turn(g):
        spread(g, x_quad, x_send.at[g], x_recv.at[g], x_peer).wait_recv()
        spread(g, x_quad, d_send.at[g, 1], d_recv.at[g, 1], y_peer, 1).start()
        spread(g, x_quad, g_send.at[g, 1], g_recv.at[g, 1], partner).start()
        spread(g, y_quad, y_send.at[g], y_recv.at[g], y_peer).wait_recv()
        spread(g, y_quad, d_send.at[g, 0], d_recv.at[g, 0], x_peer, 0).start()
        spread(g, y_quad, g_send.at[g, 2], g_recv.at[g, 2], partner).start()

    def corner(g):
        spread(g, d_quad, d_send.at[g, 0], d_recv.at[g, 0], x_peer, 0).wait_recv()
        spread(g, d_quad, d_send.at[g, 1], d_recv.at[g, 1], y_peer, 1).wait_recv()
        spread(g, d_quad, g_send.at[g, 3], g_recv.at[g, 3], partner).start()

    def put(g, m, core):
        return pltpu.make_async_copy(full.at[g, m, core], chunk(outs, g, 0, m, core, rows), out_sem.at[g, m, core])

    for g in range(GROUPS):
        swirl(g)
    for g in range(GROUPS):
        turn(g)
    for k in range(1, shards):
        remote(vec_sum.at[shard], vec_last.at[k - 1], v_send.at[2 + k], v_recv.at[2 + k], z_peers[k - 1]).wait()
    total = vec_sum[shard]
    for k in range(shards - 1):
        total = total + vec_last[k]
    vec_ring[0] = total
    for k in range(1, quads):
        remote(vec_ring.at[0], vec_ring.at[quads - k], v_send.at[2 + shards + k], v_recv.at[2 + shards + quads - k], q_peers[k - 1]).start()
    for k in range(1, quads):
        remote(vec_ring.at[0], vec_ring.at[k], v_send.at[2 + shards + k], v_recv.at[2 + shards + k], q_peers[k - 1]).wait()
        total = total + vec_ring[k]
    vec_out[...] = total
    for g in range(GROUPS):
        corner(g)
    for g in range(GROUPS):
        for i, member in enumerate((quad, x_quad, y_quad, d_quad)):
            spread(g, member, g_send.at[g, i], g_recv.at[g, i], partner, core=1 - side).wait_recv()
        for m in range(4):
            for core in range(2):
                put(g, m, core).start()
    for g in range(GROUPS):
        for m in range(4):
            for core in range(2):
                put(g, m, core).wait()

        def drain(f, carry, g=g):
            for m in range(4):
                c_copy(g, f, m).wait_send()
            return carry
        lax.fori_loop(0, shards, drain, 0)
        for k in range(1, shards):
            z_copy(g, k).wait_send()
        spread(g, quad, x_send.at[g], x_recv.at[g], x_peer).wait_send()
        spread(g, quad, y_send.at[g], y_recv.at[g], y_peer).wait_send()
        spread(g, y_quad, d_send.at[g, 0], d_recv.at[g, 0], x_peer, 0).wait_send()
        spread(g, x_quad, d_send.at[g, 1], d_recv.at[g, 1], y_peer, 1).wait_send()
        for i in range(4):
            spread(g, quad, g_send.at[g, i], g_recv.at[g, i], partner).wait_send()
    vec_copies[0].wait_send()


def reduce_grads(shards, quads, qkvo, up, down, vec):
    model, hidden = up.shape
    rows = model // shards // 2
    any_space = pl.BlockSpec(memory_space=pl.ANY)
    vmem_space = pl.BlockSpec(memory_space=pltpu.VMEM)
    dma = pltpu.SemaphoreType.DMA
    low = jnp.bfloat16
    wide = jnp.float32
    piece = (rows, model)
    vec_one = vec.shape[1:]
    spare = max(quads - 1, 1)
    return pl.pallas_call(
        functools.partial(reduce_body, shards, quads, rows),
        name="reduce_grads",
        out_shape=(
            jax.ShapeDtypeStruct((4, 2 * rows, model), low),
            jax.ShapeDtypeStruct((2 * rows, hidden), low),
            jax.ShapeDtypeStruct((8 * rows, model), low),
            jax.ShapeDtypeStruct(vec_one, wide),
        ),
        in_specs=[any_space] * 3 + [vmem_space],
        out_specs=(any_space,) * 3 + (vmem_space,),
        scratch_shapes=[
            pltpu.VMEM((GROUPS, shards, 4) + piece, low),
            pltpu.VMEM((GROUPS, shards, 4) + piece, low),
            pltpu.VMEM((GROUPS, shards, 2) + piece, low),
            pltpu.VMEM((GROUPS, shards) + piece, low),
            pltpu.VMEM((GROUPS, shards - 1) + piece, low),
            pltpu.VMEM((GROUPS, spare) + piece, low),
            pltpu.VMEM((GROUPS, 4, 2) + piece, low),
            pltpu.VMEM(vec.shape, wide),
            pltpu.VMEM((3,) + vec.shape, wide),
            pltpu.VMEM((shards - 1,) + vec_one, wide),
            pltpu.VMEM((quads,) + vec_one, wide),
            dma((GROUPS, shards, 4)),
            dma((GROUPS, shards, 4)), dma((GROUPS, shards, 4)),
            dma((GROUPS, shards, 2)), dma((GROUPS, shards, 2)),
            dma((GROUPS, shards)), dma((GROUPS, shards)),
            dma((GROUPS, shards - 1)), dma((GROUPS, shards - 1)),
            dma((GROUPS, spare)), dma((GROUPS, spare)),
            dma((GROUPS,)), dma((GROUPS,)), dma((GROUPS,)), dma((GROUPS,)),
            dma((GROUPS, 2)), dma((GROUPS, 2)),
            dma((GROUPS, 4)), dma((GROUPS, 4)),
            dma((GROUPS, 4, 2)),
            dma((3 + shards + quads,)), dma((3 + shards + quads,)),
        ],
        compiler_params=pltpu.CompilerParams(
            collective_id=1, has_side_effects=True, vmem_limit_bytes=60_000_000
        ),
    )(qkvo, up, down, vec)


def layer_norm(values, gain, offset):
    centre = values - jnp.mean(values, axis=-1, keepdims=True)
    scale = lax.rsqrt(jnp.mean(centre * centre, axis=-1, keepdims=True) + norm_eps)
    unit = centre * scale
    return unit, scale, (unit * gain + offset).astype(jnp.bfloat16)


def norm_back(upstream, unit, scale, gain):
    scaled = upstream * gain
    mean_one = jnp.mean(scaled, axis=-1, keepdims=True)
    mean_two = jnp.mean(scaled * unit, axis=-1, keepdims=True)
    return (
        scale * (scaled - mean_one - unit * mean_two),
        jnp.sum(upstream * unit, axis=0),
        jnp.sum(upstream, axis=0),
    )


def on_device(
    shards, quads,
    layer_input, segment, rand_blocks, first_gain, first_bias, query_weight, query_bias,
    key_weight, value_weight, value_bias, out_weight, out_bias, second_gain, second_bias,
    up_weight, up_bias, down_weight, down_bias, cotangent,
):
    micro, _, half, model = layer_input.shape
    side = lax.axis_index("seq")
    rows = micro * half
    part = model // shards
    low, wide = jnp.bfloat16, jnp.float32
    vec = jnp.stack(
        [first_gain, first_bias, query_bias, value_bias, out_bias, second_gain, second_bias, down_bias]
        + [up_bias[i * part:(i + 1) * part] for i in range(4)]
    )
    vec = jnp.pad(vec, ((0, 4), (0, 256 - part)))
    w_qkvo, w_up, w_down, vec_all = gather_weights(
        shards, jnp.stack([query_weight, key_weight, value_weight, out_weight]), up_weight, down_weight, vec
    )
    vec_all = vec_all[:, :, :part].astype(wide)
    flat = jnp.moveaxis(vec_all[:, :8], 0, 1).reshape(8, model)
    gain_one, bias_one, b_query, b_value, b_out, gain_two, bias_two, b_down = [flat[i] for i in range(8)]
    b_up = vec_all[:, 8:12].reshape(4 * model)
    span, aug_own, aug_other, block_bias, doc_bias = tables(segment[:, 0], rand_blocks[:, 0], side, half)

    tokens = layer_input.reshape(rows, model).astype(wide)
    unit_one, scale_one, normed = layer_norm(tokens, gain_one, bias_one)
    swap = [(0, 1), (1, 0)]
    keys = nn(normed, w_qkvo[1]).astype(low)
    keys_other = lax.ppermute(keys, "seq", swap)
    values = (nn(normed, w_qkvo[2]) + b_value).astype(low)
    values_other = lax.ppermute(values, "seq", swap)
    queries = (nn(normed, w_qkvo[0]) + b_query).astype(low)
    cut = lambda array: array.reshape(micro, half, model)
    attended = (span, cut(queries), cut(keys), cut(values), cut(keys_other), cut(values_other),
                aug_own, aug_other, block_bias, doc_bias)
    mixed, lse = attend_forward(*attended)
    mixed_rows = mixed.reshape(rows, model)
    middle = tokens + nn(mixed_rows, w_qkvo[3]) + b_out
    unit_two, scale_two, normed_two = layer_norm(middle, gain_two, bias_two)
    inner = nn(normed_two, w_up) + b_up
    phi = 0.5 * (1.0 + lax.erf(inner * 0.7071067811865476))
    hidden = (inner * phi).astype(low)
    slope = phi + inner * (jnp.exp(-0.5 * inner * inner) * 0.3989422804014327)
    result = (middle + nn(hidden, w_down) + b_down).astype(low)

    branch = cotangent.reshape(rows, model)
    upstream = branch.astype(wide)
    d_down = tn(hidden, branch).astype(low)
    grad_inner = (nt(branch, w_down) * slope).astype(low)
    d_up = tn(normed_two, grad_inner).astype(low)
    grad_two, d_gain_two, d_bias_two = norm_back(nt(grad_inner, w_up), unit_two, scale_two, gain_two)
    grad_middle = upstream + grad_two
    grad_attn = grad_middle.astype(low)
    d_out = tn(mixed_rows, grad_attn).astype(low)
    grad_mixed = nt(grad_attn, w_qkvo[3]).astype(low)
    d_query, d_key, d_value, d_key_other, d_value_other = attend_backward(*attended, mixed, cut(grad_mixed), lse)
    join = lambda own, other: (
        own.reshape(rows, model).astype(wide) + lax.ppermute(other.reshape(rows, model), "seq", swap).astype(wide)
    ).astype(low)
    d_query = d_query.reshape(rows, model)
    d_key = join(d_key, d_key_other)
    d_value = join(d_value, d_value_other)
    grad_normed = nt(d_query, w_qkvo[0]) + nt(d_key, w_qkvo[1]) + nt(d_value, w_qkvo[2])
    grad_one, d_gain_one, d_bias_one = norm_back(grad_normed, unit_one, scale_one, gain_one)
    input_grad = (grad_middle + grad_one).astype(low)
    d_qkvo = jnp.stack([tn(normed, d_query), tn(normed, d_key), tn(normed, d_value), d_out.astype(wide)]).astype(low)
    total = lambda array: jnp.sum(array.astype(wide), axis=0)
    small = jnp.stack([d_gain_one, d_bias_one, total(d_query), total(d_value), total(grad_attn),
                       d_gain_two, d_bias_two, total(branch)])
    small = jnp.moveaxis(small.reshape(8, shards, part), 1, 0)
    small = jnp.concatenate([small, total(grad_inner).reshape(shards, 4, part)], axis=1)
    small = jnp.pad(small, ((0, 0), (0, 4), (0, 256 - part)))
    g_qkvo, g_up, g_down, g_vec = reduce_grads(shards, quads, d_qkvo, d_up, d_down, small)
    g_qkvo, g_up, g_down = g_qkvo.astype(wide), g_up.astype(wide), g_down.astype(wide)
    g_vec = g_vec[:, :part]
    shape = layer_input.shape
    return (
        result.reshape(shape), input_grad.reshape(shape), g_vec[0], g_vec[1], g_qkvo[0], g_vec[2],
        g_qkvo[1], g_qkvo[2], g_vec[3], g_qkvo[3], g_vec[4], g_vec[5], g_vec[6], g_up,
        g_vec[8:12].reshape(4 * part), g_down, g_vec[7],
    )


def solution(mesh):
    row = P(None, ("rep", "fsdp"), "seq", None)
    flat, wide = P("fsdp"), P("fsdp", None)
    shards, quads = mesh.shape["fsdp"], mesh.shape["rep"] // 4
    assert mesh.shape["seq"] == 2 and mesh.shape["rep"] % 4 == 0
    return jax.shard_map(
        functools.partial(on_device, shards, quads),
        mesh=mesh,
        in_specs=(
            row, P(None, ("rep", "fsdp"), None), P(None, ("rep", "fsdp"), None, None, None),
            flat, flat, wide, flat, wide, wide, flat, wide, flat, flat, flat, wide, flat, wide, flat, row,
        ),
        out_specs=(row, row, flat, flat, wide, flat, wide, wide, flat, wide, flat, flat, flat, wide, flat, wide, flat),
        check_vma=False,
    )
```

time: 1370 us -> 387 us (0.28)
  waiting for transfers between devices: 665 us -> 0.01 us
  matrix products: 353 us -> 101 us
  Pallas kernels: 0 us -> 230 us
  local copies, waits for them, and re-layouts: 192 us -> 16.6 us
  blocking collectives: 55.9 us -> 0 us
  other arithmetic: 75.3 us -> 29.8 us
  between operations: 17.9 us -> 1.65 us
    reduce_scatter x16 -> x0, waiting for transfers between devices: 505 us -> none  [the longest x2 174 us: on_device(): lax.psum_scatter(grad_list[11].astype(jnp.bfloat16), 'fsdp', scatter_dime...]
    dot_general x120 -> x18, matrix products: 353 us -> 101 us  [the longest x6 37.5 us: nn(): return jnp.dot(a, b, preferred_element_type=jnp.float32)]
    pallas_call x0 -> x4, Pallas kernels: none -> 230 us  [the longest x1 111 us: reduce_grads(): pl.pallas_call(functools.partial(reduce_body, shards, quads, rows), name=...]
    reshape x24 -> x3, local copies, waits for them, and re-layouts: 113 us -> 0.76 us  [the longest x1 0.67 us: on_device(): g_vec[8:12].reshape(4 * part)]
    all_gather x10 -> x0, waiting for transfers between devices: 91.8 us -> none  [the longest x1 30.6 us: on_device(): lax.all_gather(shards[13], 'fsdp', axis=0, tiled=True)]
    psum x1 -> x0, waiting for transfers between devices: 62.8 us -> none  [on_device(): lax.psum(as_sent(collected), ('rep', 'seq'))]
    unnamed x2 -> x0, blocking collectives: 29.7 us -> none
    unnamed x214 -> x67, local copies, waits for them, and re-layouts: 21.2 us -> 2.14 us
  transfers between devices with their start and end apart: 27 -> 4, of which waited for: 19 -> 0; matrix products, arithmetic and copies ran while one was open for 33% -> 14% of each run, Pallas kernels for 0% -> 0%
where the time goes in v1:
time: 387 us; the launch traced here: 381 us
  Pallas kernels  230 us (59%)
  matrix products  101 us (26%)
  other arithmetic  29.8 us (8%)
  local copies, waits for them, and re-layouts  16.6 us (4%)
    pallas_call x1, Pallas kernels, reduce_grads(): pl.pallas_call(functools.partial(reduce_body, shards, quads, rows), name=...  111 us
    pallas_call x1, Pallas kernels, gather_weights(): pl.pallas_call(functools.partial(gather_body, shards, rows), name='gather...  68.3 us
    dot_general x6, matrix products, nn(): return jnp.dot(a, b, preferred_element_type=jnp.float32)  37.5 us
    dot_general x6, matrix products, nt(): lax.dot_general(a, b, (((1,), (1,)), ((), ())), preferred_element_type=jn...  32.6 us
    dot_general x6, matrix products, tn(): lax.dot_general(a, b, (((0,), (0,)), ((), ())), preferred_element_type=jn...  31.1 us
    pallas_call x1, Pallas kernels, attend_backward(): pl.pallas_call(backward_body, name='attend_backward', out_shape=(shape,)...  30.6 us
    pallas_call x1, Pallas kernels, attend_forward(): pl.pallas_call(forward_body, name='attend_forward', out_shape=(jax.ShapeD...  20.5 us
  transfers between devices with their start and end apart: 4, of which 0 were waited for; matrix products, arithmetic and copies ran while one was open for 14% of the time, Pallas kernels for 0%

profile of v1, /device:TPU:25, one launch (start us, length us, event | category | flops | bytes accessed | tf_op | source)
XLA Modules:
  0.0 380.6 jit_solution(3459137110028136434)
XLA Ops:
  7.6 2.4 pad_maximum_fusion.1.qkvo_in
  10.0 68.3 %gather_weights.1 = (bf16[4,768,768]{2,1,0:T(8,128)(2,1)}, bf16[768,3072]{1,0:T(8,128)(2,1)}, bf16[3072,768]{1,0:T(8,128)(2,1)}, bf16[4,16,256]{2,1,0:T(8,128)(2,1)}) custom-call(bf16[4,192,768]{2,1,0:T(8,128)(2,1)} %pad_maximum_fusion.1.qkvo_in, bf16[192,3072]{1,0:T(8,128)(2,1)} %up_in.1, bf16[768,768]{1,0:T(8,128)(2,1)} %down_in.1, bf16[16,256]{1,0:T(8,128)(2,1)} %pad.8.vec_in), custom_call_target="tpu_custom_call" | custom-call | tf_op jit(solution)/shard_map/gather_weights/pallas_call | solution.py:412
  81.0 4.4 %add_convert_fusion.2 = bf16[1024,768]{1,0:T(8,128)(2,1)} fusion(bf16[1024,768]{1,0:T(8,128)(2,1)S(1)} %bitcast.169, f32[768]{0:T(1024)S(1)} %add.290, bf16[4,768,768]{2,1,0:T(8,128)(2,1)} %get-tuple-element.33), kind=kOutput, calls=%fused_computation.52 | convolution fusion | flops 1209532416 | bytes 4328448 | tf_op jit(solution)/shard_map/dot_general | solution.py:28
  85.4 3.9 %convolution_convert_fusion.3 = bf16[1024,768]{1,0:T(8,128)(2,1)} fusion(bf16[1024,768]{1,0:T(8,128)(2,1)S(1)} %bitcast.170, bf16[4,768,768]{2,1,0:T(8,128)(2,1)} %get-tuple-element.33), kind=kOutput, calls=%fused_computation.58 | convolution fusion | flops 1208745984 | bytes 4325376 | tf_op jit(solution)/shard_map/dot_general | solution.py:28
  98.6 4.3 %add_convert_fusion.3 = bf16[1024,768]{1,0:T(8,128)(2,1)} fusion(bf16[1024,768]{1,0:T(8,128)(2,1)} %bitcast.171, f32[768]{0:T(1024)S(1)} %add.287, bf16[4,768,768]{2,1,0:T(8,128)(2,1)} %get-tuple-element.33), kind=kOutput, calls=%fused_computation.53 | convolution fusion | flops 1209532416 | bytes 4328448 | tf_op jit(solution)/shard_map/dot_general | solution.py:28
  102.9 20.5 %attend_forward.1 = (bf16[2,512,768]{2,1,0:T(8,128)(2,1)}, f32[2,6,2,512]{3,2,1,0:T(2,128)}) custom-call(s32[2,2,4]{2,1,0:T(2,128)} %pad_add_fusion.span_ref, bf16[2,512,768]{2,1,0:T(8,128)(2,1)} %bitcast.206, bf16[2,512,768]{2,1,0:T(8,128)(2,1)} %bitcast.14.ko_ref, bf16[2,512,768]{2,1,0:T(8,128)(2,1)} %bitcast.16.vo_ref, ...), custom_call_target="tpu_custom_call" | custom-call | flops 20000000000 | bytes 20000000 | tf_op jit(solution)/shard_map/attend_forward/pallas_call | solution.py:191
  123.4 3.5 fusion.85
  127.5 11.9 %multiply_convert_fusion = (bf16[1024,3072]{1,0:T(8,128)(2,1)}, f32[1024,3072]{1,0:T(8,128)}) fusion(f32[3072]{0:T(1024)S(1)} %add.313, bf16[768,3072]{1,0:T(8,128)(2,1)S(1)} %bitcast.200, f32[1024,768]{1,0:T(8,128)S(1)} %get-tuple-element.175, f32[768]{0:T(1024)S(1)} %add.310, f32[768]{0:T(1024)S(1)} %mul.173, f32[1024]{0:T(1024)S(1)} %add_rsqrt_fusion, ...), kind=kOutput, calls=%fused_computation.8 | convolution fusion | flops 4854644736 | bytes 26765312 | tf_op jit(solution)/shard_map/dot_general | solution.py:28
  139.4 12.1 %convert_reduce_fusion = (f32[3072]{0:T(1024)S(1)}, bf16[1024,3072]{1,0:T(8,128)(2,1)S(1)}) fusion(f32[1024,3072]{1,0:T(8,128)} %get-tuple-element.179, f32[3072]{0:T(1024)S(1)} %add.313, bf16[3072,768]{1,0:T(8,128)(2,1)S(1)} %bitcast.198, bf16[1024,768]{1,0:T(8,128)(2,1)S(1)} %bitcast.167), kind=kOutput, calls=%fused_computation.7 | convolution fusion | flops 4872729600 | bytes 25190400 | tf_op jit(solution)/shard_map/dot_general | solution.py:20
  151.5 5.8 %multiply_reduce_fusion = (f32[768]{0:T(1024)S(1)}, f32[1024]{0:T(1024)S(1)}, f32[1024]{0:T(1024)S(1)}, f32[768]{0:T(1024)S(1)}, f32[1024,768]{1,0:T(8,128)S(1)}) fusion(f32[1024,768]{1,0:T(8,128)S(1)} %get-tuple-element.175, f32[1024]{0:T(1024)S(1)} %add_rsqrt_fusion, f32[1024]{0:T(1024)S(1)} %broadcast_multiply_fusion.4, f32[768]{0:T(1024)S(1)} %mul.173, ...), kind=kOutput, calls=%fused_computation.42 | convolution fusion | flops 4838912000 | bytes 17327104 | tf_op jit(solution)/shard_map/dot_general | solution.py:20
  157.3 8.0 %convolution_convert_fusion.1.up_in = bf16[768,3072]{1,0:T(8,128)(2,1)} fusion(bf16[1024,3072]{1,0:T(8,128)(2,1)S(1)} %get-tuple-element.181, f32[1024,768]{1,0:T(8,128)S(1)} %get-tuple-element.175, f32[768]{0:T(1024)S(1)} %add.310, f32[768]{0:T(1024)S(1)} %mul.173, f32[1024]{0:T(1024)S(1)} %add_rsqrt_fusion, f32[1024]{0:T(1024)S(1)} %broadcast_multiply_fusion.4), kind=kOutput, calls=%fused_computation.11 | convolution fusion | flops 4838129664 | bytes 14170112 | tf_op jit(solution)/shard_map/dot_general | solution.py:24
  166.8 4.8 %convolution_convert_fusion.2 = bf16[1024,768]{1,0:T(8,128)(2,1)} fusion(bf16[4,768,768]{2,1,0:T(8,128)(2,1)} %get-tuple-element.33, f32[1024,768]{1,0:T(8,128)S(1)} %get-tuple-element.136), kind=kOutput, calls=%fused_computation.57 | convolution fusion | flops 1209532416 | bytes 5898240 | tf_op jit(solution)/shard_map/dot_general | solution.py:20
  171.6 30.6 %attend_backward.1 = (bf16[2,512,768]{2,1,0:T(8,128)(2,1)}, bf16[2,512,768]{2,1,0:T(8,128)(2,1)}, bf16[2,512,768]{2,1,0:T(8,128)(2,1)}, bf16[2,512,768]{2,1,0:T(8,128)(2,1)}, bf16[2,512,768]{2,1,0:T(8,128)(2,1)}) custom-call(s32[2,2,4]{2,1,0:T(2,128)} %pad_add_fusion.span_ref, bf16[2,512,768]{2,1,0:T(8,128)(2,1)} %bitcast.207, ...), custom_call_target="tpu_custom_call" | custom-call | flops 40000000000 | bytes 40000000 | tf_op jit(solution)/shard_map/attend_backward/pallas_call | solution.py:216
  202.8 10.1 %convolution_convert_fusion.down_in = bf16[3072,768]{1,0:T(8,128)(2,1)} fusion(bf16[1024,3072]{1,0:T(8,128)(2,1)} %get-tuple-element.178, bf16[1024,768]{1,0:T(8,128)(2,1)S(1)} %bitcast.168), kind=kOutput, calls=%fused_computation.10 | convolution fusion | flops 4834197504 | bytes 12582912 | tf_op jit(solution)/shard_map/dot_general | solution.py:24
  212.9 9.5 %add_convert_fusion = bf16[1024,768]{1,0:T(8,128)(2,1)} fusion(f32[1024,768]{1,0:T(8,128)S(1)} %copy-done.4, bf16[1024,3072]{1,0:T(8,128)(2,1)} %get-tuple-element.178, bf16[3072,768]{1,0:T(8,128)(2,1)} %get-tuple-element.36, f32[768]{0:T(1024)S(1)} %add.319), kind=kOutput, calls=%fused_computation.49 | convolution fusion | flops 4834197504 | bytes 15731712 | tf_op jit(solution)/shard_map/dot_general | solution.py:28
  222.4 4.5 %fusion.39 = f32[1024,768]{1,0:T(8,128)} fusion(bf16[1024,768]{1,0:T(8,128)(2,1)S(1)} %bitcast.174, bf16[4,768,768]{2,1,0:T(8,128)(2,1)} %get-tuple-element.33), kind=kOutput, calls=%fused_computation.75 | convolution fusion | flops 1207959552 | bytes 5898240 | tf_op jit(solution)/shard_map/dot_general | solution.py:20
  227.6 4.1 %fusion.28 = bf16[1,768,768]{2,1,0:T(8,128)(2,1)} fusion(bf16[1024,768]{1,0:T(8,128)(2,1)S(1)} %bitcast.172, bf16[1024,768]{1,0:T(8,128)(2,1)} %bitcast.173), kind=kOutput, calls=%fused_computation.63 | convolution fusion | flops 1208549376 | bytes 4325376 | tf_op jit(solution)/shard_map/dot_general | solution.py:24
  231.7 4.0 %fusion.31 = bf16[1,768,768]{2,1,0:T(8,128)(2,1)} fusion(bf16[1024,768]{1,0:T(8,128)(2,1)} %bitcast.205, f32[1024,768]{1,0:T(8,128)S(1)} %copy-done.6), kind=kOutput, calls=%fused_computation.66 | convolution fusion | flops 1209335808 | bytes 5898240 | tf_op jit(solution)/shard_map/dot_general | solution.py:24
  241.4 4.0 %fusion.27 = (f32[768]{0:T(1024)S(1)}, f32[1024]{0:T(1024)S(1)}, f32[1024]{0:T(1024)S(1)}, f32[768]{0:T(1024)S(1)}, bf16[1024,768]{1,0:T(8,128)(2,1)S(1)}, /*index=5*/f32[1024,768]{1,0:T(8,128)}) fusion(bf16[2,1,512,768]{3,2,1,0:T(8,128)(2,1)S(1)} %copy-done.2, f32[1024]{0:T(1024)S(1)} %bitcast.185, f32[1024]{0:T(1024)S(1)} %bitcast.183, ...), kind=kOutput, calls=%fused_computation.40 | convolution fusion | flops 1219752448 | bytes 15366144 | tf_op jit(solution)/shard_map/dot_general | solution.py:20
  245.5 2.5 fusion.29
  247.9 2.5 fusion.30
  251.3 3.9 %pad_maximum_fusion.qkvo_in = bf16[4,768,768]{2,1,0:T(8,128)(2,1)} fusion(bf16[1,768,768]{2,1,0:T(8,128)(2,1)} %fusion.31, bf16[1,768,768]{2,1,0:T(8,128)(2,1)} %fusion.30, bf16[1,768,768]{2,1,0:T(8,128)(2,1)} %fusion.29, bf16[1,768,768]{2,1,0:T(8,128)(2,1)S(1)} %copy-done.13), kind=kLoop, calls=%fused_computation.12 | loop fusion | flops 7077888 | bytes 9437184 | tf_op jit(solution)/shard_map/stack | solution.py:776
  255.3 110.9 %reduce_grads.1 = (bf16[4,192,768]{2,1,0:T(8,128)(2,1)}, bf16[192,3072]{1,0:T(8,128)(2,1)}, bf16[768,768]{1,0:T(8,128)(2,1)}, f32[16,256]{1,0:T(8,128)}) custom-call(bf16[4,768,768]{2,1,0:T(8,128)(2,1)} %pad_maximum_fusion.qkvo_in, bf16[768,3072]{1,0:T(8,128)(2,1)} %convolution_convert_fusion.1.up_in, bf16[3072,768]{1,0:T(8,128)(2,1)} %convolution_convert_fusion.down_in, ...), custom_call_target="tpu_custom_call" | custom-call | tf_op jit(solution)/shard_map/reduce_grads/pallas_call | solution.py:651
  375.8 4.3 %fusion.24 = bf16[1024,768]{1,0:T(8,128)(2,1)} fusion(f32[1024,768]{1,0:T(8,128)} %copy-done.5, bf16[2,1,512,768]{3,2,1,0:T(8,128)(2,1)S(1)} %copy-done.2, f32[1024,768]{1,0:T(8,128)} %get-tuple-element.177, f32[1024]{0:T(1024)S(1)} %broadcast_multiply_fusion, f32[1024]{0:T(1024)S(1)} %bitcast.186, f32[1024]{0:T(1024)S(1)} %broadcast_multiply_fusion.1, ...), kind=kLoop, calls=%fused_computation.37 | loop fusion | flops 7864320 | bytes 9456640 | tf_op jit(solution)/shard_map/convert_element_type | solution.py:775
  (173 shorter events, 38.2 us)
Async XLA Ops:
  0.7 90.2 %copy-start = (s32[2,1,12,16,3]{3,1,4,2,0:T(1,128)S(1)}, s32[2,1,12,16,3]{3,1,4,2,0:T(1,128)}, u32[]{:S(2)}) copy-start(s32[2,1,12,16,3]{3,1,4,2,0:T(1,128)} %param.21) | copy-start | bytes 13828
  0.7 78.7 %copy-start.2 = (bf16[2,1,512,768]{3,2,1,0:T(8,128)(2,1)S(1)}, bf16[2,1,512,768]{3,2,1,0:T(8,128)(2,1)}, u32[]{:S(2)}) copy-start(bf16[2,1,512,768]{3,2,1,0:T(8,128)(2,1)} %param.19) | copy-start | bytes 4718596
  81.0 4.4 %copy-start.8 = (bf16[2,1,512,768]{3,2,1,0:T(8,128)(2,1)}, bf16[2,1,512,768]{3,2,1,0:T(8,128)(2,1)S(1)}, u32[]{:S(2)}) copy-start(bf16[2,1,512,768]{3,2,1,0:T(8,128)(2,1)S(1)} %fusion.13) | copy-start | bytes 4718596
  85.4 4.4 %copy-start.18 = (s32[2,1,1024]{2,1,0:T(1,128)S(1)}, s32[2,1,1024]{2,1,0:T(1,128)}, u32[]{:S(2)}) copy-start(s32[2,1,1024]{2,1,0:T(1,128)} %param.20) | copy-start | bytes 24580
  85.4 5.8 %copy-start.7 = (bf16[2,1,512,768]{3,2,1,0:T(8,128)(2,1)S(1)}, bf16[2,1,512,768]{3,2,1,0:T(8,128)(2,1)}, u32[]{:S(2)}) copy-start(bf16[2,1,512,768]{3,2,1,0:T(8,128)(2,1)} %param.37) | copy-start | bytes 4718596
  85.4 17.5 %collective-permute-start.1 = (bf16[1024,768]{1,0:T(8,128)(2,1)}, bf16[1024,768]{1,0:T(8,128)(2,1)}, u32[]{:S(2)}, u32[]{:S(2)}) collective-permute-start(bf16[1024,768]{1,0:T(8,128)(2,1)} %add_convert_fusion.2), channel_id=1, source_target_pairs={{0,1},{1,0},{2,3},{3,2},{4,5},{5,4},{6,7},{7,6},{8,9},{9,8},{10,11... | collective-permute-start | bytes 4718600 | tf_op jit(solution)/shard_map/ppermute | solution.py:741
  89.3 13.6 %collective-permute-start = (bf16[1024,768]{1,0:T(8,128)(2,1)}, bf16[1024,768]{1,0:T(8,128)(2,1)}, u32[]{:S(2)}, u32[]{:S(2)}) collective-permute-start(bf16[1024,768]{1,0:T(8,128)(2,1)} %convolution_convert_fusion.3), channel_id=1, source_target_pairs={{0,1},{1,0},{2,3},{3,2},{4,5},{5,4},{6,7},{7,6},{8,9},{9,8},{10,11... | collective-permute-start | bytes 4718600 | tf_op jit(solution)/shard_map/ppermute | solution.py:739
  123.4 4.0 %slice-start.4 = ((s8[4718592]{0:T(1024)(128)(4,1)}), s8[4194304]{0:T(1024)(128)(4,1)S(1)}, s32[]{:S(2)}) async-start(s8[4718592]{0:T(1024)(128)(4,1)} %bitcast.199), calls=%async_computation.4 | async-start | bytes 8388608
  123.4 4.0 %slice-start.5 = ((s8[4718592]{0:T(1024)(128)(4,1)}), s8[524288]{0:T(1024)(128)(4,1)S(1)}, s32[]{:S(2)}) async-start(s8[4718592]{0:T(1024)(128)(4,1)} %bitcast.199), calls=%async_computation.5 | async-start | bytes 1048576
  126.9 38.4 %copy-start.3 = (f32[1024,768]{1,0:T(8,128)}, f32[1024,768]{1,0:T(8,128)S(1)}, u32[]{:S(2)}) copy-start(f32[1024,768]{1,0:T(8,128)S(1)} %get-tuple-element.175) | copy-start | bytes 9437188
  126.9 12.5 %slice-start.2 = ((s8[4718592]{0:T(1024)(128)(4,1)}), s8[4194304]{0:T(1024)(128)(4,1)S(1)}, s32[]{:S(2)}) async-start(s8[4718592]{0:T(1024)(128)(4,1)} %bitcast.197), calls=%async_computation.2 | async-start | bytes 8388608
  127.5 11.9 %slice-start.3 = ((s8[4718592]{0:T(1024)(128)(4,1)}), s8[524288]{0:T(1024)(128)(4,1)S(1)}, s32[]{:S(2)}) async-start(s8[4718592]{0:T(1024)(128)(4,1)} %bitcast.197), calls=%async_computation.3 | async-start | bytes 1048576
  166.8 4.8 %copy-start.5 = (f32[1024,768]{1,0:T(8,128)}, f32[1024,768]{1,0:T(8,128)S(1)}, u32[]{:S(2)}) copy-start(f32[1024,768]{1,0:T(8,128)S(1)} %get-tuple-element.136) | copy-start | bytes 9437188
  202.2 33.6 %collective-permute-start.2 = (bf16[1024,768]{1,0:T(8,128)(2,1)}, bf16[1024,768]{1,0:T(8,128)(2,1)}, u32[]{:S(2)}, u32[]{:S(2)}) collective-permute-start(bf16[1024,768]{1,0:T(8,128)(2,1)} %bitcast.202), channel_id=1, source_target_pairs={{0,1},{1,0},{2,3},{3,2},{4,5},{5,4},{6,7},{7,6},{8,9},{9,8},{10,11... | collective-permute-start | bytes 4718600 | tf_op jit(solution)/shard_map/ppermute | solution.py:768
  202.4 36.7 %collective-permute-start.3 = (bf16[1024,768]{1,0:T(8,128)(2,1)}, bf16[1024,768]{1,0:T(8,128)(2,1)}, u32[]{:S(2)}, u32[]{:S(2)}) collective-permute-start(bf16[1024,768]{1,0:T(8,128)(2,1)} %bitcast.201), channel_id=1, source_target_pairs={{0,1},{1,0},{2,3},{3,2},{4,5},{5,4},{6,7},{7,6},{8,9},{9,8},{10,11... | collective-permute-start | bytes 4718600 | tf_op jit(solution)/shard_map/ppermute | solution.py:768
  202.8 10.1 %copy-start.4 = (f32[1024,768]{1,0:T(8,128)S(1)}, f32[1024,768]{1,0:T(8,128)}, u32[]{:S(2)}) copy-start(f32[1024,768]{1,0:T(8,128)} %copy-done.3) | copy-start | bytes 9437188
  212.9 9.5 %copy-start.10 = (bf16[2,512,768]{2,1,0:T(8,128)(2,1)S(1)}, bf16[2,512,768]{2,1,0:T(8,128)(2,1)}, u32[]{:S(2)}) copy-start(bf16[2,512,768]{2,1,0:T(8,128)(2,1)} %get-tuple-element.38) | copy-start | bytes 4718596
  222.4 5.2 %copy-start.9 = (bf16[2,1,512,768]{3,2,1,0:T(8,128)(2,1)S(1)}, bf16[2,1,512,768]{3,2,1,0:T(8,128)(2,1)}, u32[]{:S(2)}) copy-start(bf16[2,1,512,768]{3,2,1,0:T(8,128)(2,1)} %copy-done.8) | copy-start | bytes 4718596
  227.6 4.1 %copy-start.6 = (f32[1024,768]{1,0:T(8,128)S(1)}, f32[1024,768]{1,0:T(8,128)}, u32[]{:S(2)}) copy-start(f32[1024,768]{1,0:T(8,128)} %copy-done.5) | copy-start | bytes 9437188
  227.6 10.0 %slice-start = ((s8[4718592]{0:T(1024)(128)(4,1)}), s8[4194304]{0:T(1024)(128)(4,1)S(1)}, s32[]{:S(2)}) async-start(s8[4718592]{0:T(1024)(128)(4,1)} %bitcast.195), calls=%async_computation | async-start | bytes 8388608
  231.7 4.1 %copy-start.12 = (bf16[2,512,768]{2,1,0:T(8,128)(2,1)S(1)}, bf16[2,512,768]{2,1,0:T(8,128)(2,1)}, u32[]{:S(2)}) copy-start(bf16[2,512,768]{2,1,0:T(8,128)(2,1)} %get-tuple-element.39) | copy-start | bytes 4718596
  231.7 5.9 %slice-start.1 = ((s8[4718592]{0:T(1024)(128)(4,1)}), s8[524288]{0:T(1024)(128)(4,1)S(1)}, s32[]{:S(2)}) async-start(s8[4718592]{0:T(1024)(128)(4,1)} %bitcast.195), calls=%async_computation.1 | async-start | bytes 1048576
  369.9 3.6 copy-start.14
  375.8 4.3 %copy-start.1 = (s32[2,1,12,16,3]{3,1,4,2,0:T(1,128)S(1)}, s32[2,1,12,16,3]{3,1,4,2,0:T(1,128)}, u32[]{:S(2)}) copy-start(s32[2,1,12,16,3]{3,1,4,2,0:T(1,128)} %param.21) | copy-start | bytes 13828
  (11 other events, 24.0 us)
